TPU v7x, 32 devices: a whole 2x2x4 slice. The times are simulated.
32 devices in a mesh: row: 8 (over z, x), col: 4 (over y, core).
Axes of the slice: x: 2, y: 2, z: 4, core: 2. Of those that a mesh axis runs over, the one named last changes fastest.
Arguments:
- amplitudes: float32 [200, 10, 10, 1024], P('row', None, None, 'col'), may hold values from -6 to 6
- old_blocks: int32 [8, 25], replicated, may hold values from 0 to 135, as said below
- old_counts: int32 [8], replicated, may hold values from 1 to 25, as said below
- new_phase: int32 [1], replicated, may hold values from 0 to 7
- fock: float32 [160, 160], P('row'), may hold values from -0.5 to 0.5
Outputs:
- contracted: float32 [16, 10, 160, 1024], P('row', None, None, 'col')
Inputs may be any that keep to these rules, and one draw needn't show every extreme that they name: `old_blocks`: over the live slots of all row devices every tile pair id 0 to 135 stands exactly once; ids in slots that are not live are arbitrary. For every residue r mod 8, at most 8 live blocks of one row device hold a tile whose index is r mod 8, and some device reaches 8 for some r. `old_counts`: the counts sum to 136; some device has exactly 25.
All inputs are finite; a program needn't handle non-finite values.
Results may differ from a plain program's by a relative error of at most 0.00007.
Values sent between devices are 32-bit elements; how exact they have to be, the bound alone decides.
No kernel may reach another device: no remote copies, remote signals or barrier semaphores. Data moves between devices by JAX's collectives and lax.ppermute only.
A program may use at most 128 MiB of HBM per device.

v0:
```python
import jax
import jax.numpy as jnp
import numpy as np
from jax import lax
from jax.sharding import PartitionSpec as P

NT = 16


def pair_table():
    table = np.zeros((NT, NT), np.int32)
    first_tile = np.zeros((NT * (NT + 1) // 2,), np.int32)
    second_tile = np.zeros((NT * (NT + 1) // 2,), np.int32)
    for first in range(NT):
        for second in range(NT):
            low = min(first, second)
            high = max(first, second)
            ident = low * NT - low * (low - 1) // 2 + (high - low)
            table[first, second] = ident
            first_tile[ident] = low
            second_tile[ident] = high
    return (table, first_tile, second_tile)


def body(amplitudes, old_blocks, old_counts, new_phase, fock):
    nrows = lax.axis_size("row")
    myself = lax.axis_index("row")
    slots = amplitudes.shape[0]
    tile = amplitudes.shape[1]
    occ_dev = amplitudes.shape[3]
    width = fock.shape[1]
    per_dev = NT // nrows
    nblocks = NT * (NT + 1) // 2
    phase = new_phase[0]
    table, first_tile, second_tile = pair_table()
    live = jnp.arange(slots, dtype=jnp.int32)[None, :] < old_counts[:, None]
    flat = amplitudes.reshape(slots, tile * tile * occ_dev)
    fock_full = lax.all_gather(fock, "row", axis=0, tiled=True)
    match_ids = old_blocks.reshape(-1)
    match_live = live.reshape(-1)
    my_ids = lax.dynamic_slice_in_dim(old_blocks, myself, 1, 0)[0]
    my_live = lax.dynamic_slice_in_dim(live, myself, 1, 0)[0]
    owner_low = (jnp.asarray(first_tile)[my_ids] + phase) % nrows
    owner_high = (jnp.asarray(second_tile)[my_ids] + phase) % nrows
    target = jnp.arange(nrows, dtype=jnp.int32)[:, None]
    sending = ((owner_low[None, :] == target) | (owner_high[None, :] == target)) & my_live[None, :]
    capacity = per_dev * ((slots - 2) // 8 + 2)
    ordinal = jnp.cumsum(sending.astype(jnp.int32), axis=1) - 1
    packing = (
        ordinal[:, None, :] == jnp.arange(capacity, dtype=jnp.int32)[None, :, None]
    ) & sending[:, None, :]
    payload = jnp.einsum(
        "dcs,sp->dcp", packing.astype(jnp.float32), flat, precision=lax.Precision.HIGHEST
    )
    filled = jnp.any(packing, axis=2)
    sent_ids = jnp.sum(jnp.where(packing, my_ids[None, None, :], 0), axis=2)
    sent_ids = jnp.where(filled, sent_ids, nblocks)
    payload_in, ids_in = (
        lax.all_to_all(payload, "row", split_axis=0, concat_axis=0, tiled=True),
        lax.all_to_all(sent_ids, "row", split_axis=0, concat_axis=0, tiled=True),
    )
    received = payload_in
    match_ids = ids_in.reshape(-1)
    match_live = match_ids < nblocks
    received = received.reshape(-1, tile * tile * occ_dev)
    index = jnp.arange(tile, dtype=jnp.int32)
    results = []
    for within in range(per_dev):
        column_tile = (myself - phase) % nrows + within * nrows
        needed = jnp.asarray(table)[:, column_tile]
        picker = ((match_ids[None, :] == needed[:, None]) & match_live[None, :]).astype(jnp.float32)
        chosen = jnp.dot(picker, received, precision=lax.Precision.HIGHEST)
        chosen = chosen.reshape(NT, tile, tile, occ_dev)
        c_global = jnp.arange(NT, dtype=jnp.int32)[:, None, None] * tile + index[None, :, None]
        b_global = column_tile * tile + index[None, None, :]
        below = (c_global < b_global)[:, :, :, None]
        above = (c_global > b_global)[:, :, :, None]
        dense = jnp.where(below, chosen, jnp.where(above, -jnp.swapaxes(chosen, 1, 2), 0.0))
        dense = dense.reshape(width, tile, occ_dev)
        outcome = jnp.einsum("ac,cbj->baj", fock_full, dense, precision=lax.Precision.HIGHEST)
        results.append(outcome)
    return jnp.stack(results, 0)


def solution(mesh):
    return jax.shard_map(
        body,
        mesh=mesh,
        in_specs=(P("row", None, None, "col"), P(), P(), P(), P("row", None)),
        out_specs=P("row", None, None, "col"),
        check_vma=False,
    )
```

profile of v0, /device:TPU:0, one launch (start us, length us, event | category | flops | bytes accessed | tf_op | source)
XLA Modules:
  0.0 239.0 jit_solution(3944722288822886608)
XLA Ops:
  0.0 0.7 fusion.30
  0.7 0.7 fusion.31
  1.4 1.4 gather_fusion
  2.8 1.4 gather_fusion.1
  4.8 0.7 iota_compare_fusion.1
  5.6 0.2 reduce_window_sum.11
  5.8 0.2 fusion.9
  6.0 0.2 select_reduce_fusion
  6.2 0.6 broadcast_select_fusion
  6.8 7.3 %all-to-all-start = ((s32[8,1,8]{2,1,0:T(1,128)}), s32[8,1,8]{2,1,0:T(1,128)S(1)}, u32[]{:S(2)}, u32[]{:S(2)}) async-start(s32[8,1,8]{2,1,0:T(1,128)} %bitcast.6), calls=%async_computation | async-start | bytes 8192 | tf_op jit(solution)/shard_map/all_to_all | solution.py:60
  14.1 5.4 %copy.19 = f32[25,10,10,256]{3,2,1,0:T(8,128)} copy(f32[25,10,10,256]{3,0,2,1:T(8,128)} %param.8) | data formatting | bytes 5120000 | tf_op args[0]
  19.5 3.2 %reshape.256 = f32[25,25600,1]{1,0,2:T(8,128)S(1)} reshape(f32[25,10,10,256]{3,2,1,0:T(8,128)} %copy.19) | data formatting | bytes 5120000 | tf_op jit(solution)/shard_map/reshape | solution.py:37
  22.7 4.6 %fusion.7 = f32[8,8,25600]{2,1,0:T(8,128)} fusion(f32[25,25600,1]{1,0,2:T(8,128)S(1)} %reshape.256, s32[8,25]{1,0:T(8,128)S(1)} %broadcast_add_fusion, pred[8,25]{1,0:T(8,128)(4,1)S(1)} %get-tuple-element.6), kind=kOutput, calls=%fused_computation.22 | convolution fusion | flops 491523200 | bytes 9114600 | tf_op jit(solution)/shard_map/dcs,sp->dcp/dot_general | solution.py:52
  27.3 0.0 copy-start.1
  27.3 0.0 all-to-all-done
  27.4 6.1 %all-to-all-start.1 = ((f32[8,8,25600]{2,1,0:T(8,128)}), f32[8,8,25600]{2,1,0:T(8,128)}, u32[]{:S(2)}, u32[]{:S(2)}) async-start(f32[8,8,25600]{2,1,0:T(8,128)} %fusion.7), calls=%async_computation.1 | async-start | bytes 13107200 | tf_op jit(solution)/shard_map/all_to_all | solution.py:59
  33.5 0.0 copy-done.1
  33.5 163.5 %all-gather = f32[8,20,160]{2,1,0:T(8,128)S(1)} all-gather(f32[1,20,160]{2,1,0:T(8,128)S(1)} %bitcast.59), channel_id=1, replica_groups=mesh['row'=8,'col'=4] {'row'}, dimensions={0}, use_global_device_ids=true | all-gather | bytes 115200 | tf_op jit(solution)/shard_map/all_gather | solution.py:38
  197.0 0.7 fusion.26
  197.7 0.1 broadcast_compare_fusion.3
  197.9 0.5 broadcast.232
  198.4 0.7 reduce.3
  199.0 0.1 eq.100
  199.1 0.0 all-to-all-done.1
  199.1 8.8 %dot_general.21 = f32[10,10,256,64]{2,1,0,3:T(8,128)} reshape(f32[25600,64]{0,1:T(8,128)} %bitcast.11) | data formatting | bytes 13107200 | tf_op jit(solution)/shard_map/dot_general | solution.py:72
  208.0 9.2 %fusion.2 = f32[16,10,10,256]{3,0,2,1:T(8,128)S(1)} fusion(f32[10,10,256,64]{2,1,0,3:T(8,128)} %dot_general.21, s32[64]{0:T(128)S(1)} %eq.100, s32[16]{0:T(128)S(1)} %get-tuple-element.13, pred[64]{0:T(512)(128)(4,1)S(1)} %broadcast_compare_fusion.4), kind=kOutput, calls=%fused_computation.4 | convolution fusion | flops 314574848 | bytes 8192384 | tf_op jit(solution)/shard_map/dot_general | solution.py:72
  217.2 0.6 fusion.5
  217.8 1.1 copy.22
  218.8 1.3 reshape.236
  220.1 9.2 %fusion = f32[16,10,10,256]{3,0,2,1:T(8,128)S(1)} fusion(f32[10,10,256,64]{2,1,0,3:T(8,128)} %dot_general.21, s32[64]{0:T(128)S(1)} %eq.100, s32[16]{0:T(128)S(1)} %get-tuple-element.14, pred[64]{0:T(512)(128)(4,1)S(1)} %broadcast_compare_fusion.4), kind=kOutput, calls=%fused_computation.2 | convolution fusion | flops 314574848 | bytes 8192384 | tf_op jit(solution)/shard_map/dot_general | solution.py:72
  229.3 0.6 fusion.4
  229.9 1.1 copy.25
  231.0 1.3 reshape.237
  232.3 0.0 copy-start
  232.3 3.2 %convolution_bitcast_fusion.1 = f32[1,10,160,256]{3,2,1,0:T(8,128)S(1)} fusion(f32[160,10,256]{2,0,1:T(8,128)} %reshape.236, f32[160,160,1]{1,0,2:T(8,128)S(1)} %reshape.258), kind=kOutput, calls=%fused_computation.14 | convolution fusion | flops 786432000 | bytes 3379200 | tf_op jit(solution)/shard_map/ac,cbj->baj/dot_general | solution.py:80
  235.4 0.0 copy-done
  235.4 1.6 convolution_bitcast_fusion
  237.0 1.9 pad_maximum_fusion
  (10 shorter events, 0.1 us)
Async XLA Ops:
  6.8 20.5 %all-to-all-start = ((s32[8,1,8]{2,1,0:T(1,128)}), s32[8,1,8]{2,1,0:T(1,128)S(1)}, u32[]{:S(2)}, u32[]{:S(2)}) async-start(s32[8,1,8]{2,1,0:T(1,128)} %bitcast.6), calls=%async_computation | async-start | bytes 8192 | tf_op jit(solution)/shard_map/all_to_all | solution.py:60
  27.3 6.1 %copy-start.1 = (f32[20,160]{1,0:T(8,128)S(1)}, f32[20,160]{1,0:T(8,128)}, u32[]{:S(2)}) copy-start(f32[20,160]{1,0:T(8,128)} %param.12) | copy-start | bytes 38404
  27.4 171.8 %all-to-all-start.1 = ((f32[8,8,25600]{2,1,0:T(8,128)}), f32[8,8,25600]{2,1,0:T(8,128)}, u32[]{:S(2)}, u32[]{:S(2)}) async-start(f32[8,8,25600]{2,1,0:T(8,128)} %fusion.7), calls=%async_computation.1 | async-start | bytes 13107200 | tf_op jit(solution)/shard_map/all_to_all | solution.py:59
  232.3 3.2 %copy-start = (f32[160,10,256]{2,0,1:T(8,128)S(1)}, f32[160,10,256]{2,0,1:T(8,128)}, u32[]{:S(2)}) copy-start(f32[160,10,256]{2,0,1:T(8,128)} %reshape.237) | copy-start | bytes 4915204
where the time goes:
time: 240 us; the launch traced here: 239 us
  blocking collectives  163 us (68%)
  matrix products  27.7 us (12%)
  local copies, waits for them, and re-layouts  27 us (11%)
  starting transfers between devices  13.4 us (6%)
  other arithmetic  6.61 us (3%)
    all_gather x1, blocking collectives, body(): fock_full = lax.all_gather(fock, 'row', axis=0, tiled=True)  163 us
    dot_general x2, matrix products, body(): chosen = jnp.dot(picker, received, precision=lax.Precision.HIGHEST)  18.3 us
    dot_general x1, local copies, waits for them, and re-layouts, body(): chosen = jnp.dot(picker, received, precision=lax.Precision.HIGHEST)  8.85 us
    all_to_all x1, starting transfers between devices, body(): lax.all_to_all(sent_ids, 'row', split_axis=0, concat_axis=0, tiled=True)  7.28 us
    all_to_all x1, starting transfers between devices, body(): lax.all_to_all(payload, 'row', split_axis=0, concat_axis=0, tiled=True)  6.13 us
    unnamed x6, local copies, waits for them, and re-layouts  5.44 us
  transfers between devices with their start and end apart: 2, of which 0 were waited for; matrix products, arithmetic and copies ran while one was open for 6% of the time, Pallas kernels for 0%

commit v1 on v0

v1 whole, which is shorter than its diff:
```python
import functools

import jax
import jax.numpy as jnp
from jax import lax
from jax.experimental import pallas as pl
from jax.experimental.pallas import tpu as pltpu
from jax.sharding import PartitionSpec as P


NT = 16
LANES = 128
VMEM_LIMIT = 60 * 2**20


class Plan:
    def __init__(self, nrows, slots):
        self.nrows = nrows
        self.half = nrows // 2
        self.per = NT // nrows
        self.cap = self.per * ((slots - 2) // 8 + 2)
        self.fwd = self.per * self.per
        self.n_send = nrows * self.cap
        self.n_fwd = (self.half - 1) * self.fwd
        self.n_loc = self.per * NT
        self.at_fwd = self.n_send
        self.at_loc = self.n_send + self.n_fwd
        self.at_level = self.at_loc + self.n_loc
        cap = self.cap
        wide = -(-5 * cap // 8), -(-6 * cap // 8), cap
        early = -(-cap // 2), -(-cap // 2), cap
        self.levels = tuple(zip(wide, early))


def route_kernel(plan, slots, ids_ref, counts_ref, phase_ref, out_ref):
    nrows, half, per, cap = plan.nrows, plan.half, plan.per, plan.cap
    me = lax.axis_index("row")
    phase = phase_ref[0]
    ids = ids_ref[...]
    first = jnp.zeros_like(ids)
    for t in range(1, NT):
        first = first + (ids >= t * NT - t * (t - 1) // 2).astype(jnp.int32)
    second = ids - (first * NT - lax.shift_right_logical(first * (first - 1), 1)) + first
    src = lax.broadcasted_iota(jnp.int32, ids.shape, 1)
    slot = lax.broadcasted_iota(jnp.int32, ids.shape, 0)
    live = slot < counts_ref[...]
    low = (first + phase) & (nrows - 1)
    high = (second + phase) & (nrows - 1)
    shift = nrows.bit_length() - 1
    w_low = lax.shift_right_logical(first, shift)
    w_high = lax.shift_right_logical(second, shift)
    pair_part = jnp.where(low < high, w_low * per + w_high, w_high * per + w_low)
    far_low = ((low ^ src) & half) != 0
    far_high = ((high ^ src) & half) != 0
    same = low == high
    one = jnp.int32(1)
    zero = jnp.int32(0)

    def flag(x):
        return jnp.where(x, one, zero)

    in_low = flag(live & ~far_low)
    in_high = flag(live & ~far_high & ~same)
    x_low = flag(live & far_low)
    x_high = flag(live & far_high & ~same)
    both = x_low * x_high
    single = x_low + x_high - 2 * both
    goal = jnp.where(x_low == 1, low, high)
    dest = lax.broadcasted_iota(jnp.int32, (nrows, nrows), 0)

    def row(x, s):
        return x[s : s + 1, :]

    def hit(x, on, s):
        return jnp.where((dest == row(x, s)) & (row(on, s) == 1), 1.0, 0.0)

    def at(mask, run):
        return jnp.sum(mask * run, axis=0, keepdims=True)

    count = jnp.zeros((nrows, nrows), jnp.float32)
    singles = []
    for s in range(slots):
        mask = hit(goal, single, s)
        singles.append(mask)
        count = count + mask
    early = jnp.zeros((nrows, nrows), jnp.float32)
    land_rows, pos_rows = [], []
    for s in range(slots):
        m_low = hit(low, both, s)
        m_high = hit(high, both, s)
        take = at(m_low, count) <= at(m_high, count)
        mask = jnp.where(take, m_low, m_high)
        pos_rows.append(at(mask, early))
        land_rows.append(jnp.where(take, row(low, s), row(high, s)))
        early = early + mask
        count = count + mask
    run = early
    for s in range(slots):
        pos_rows[s] = pos_rows[s] + at(singles[s], run)
        run = run + singles[s]
    run_in = jnp.zeros((nrows, nrows), jnp.float32)
    low_rows, high_rows = [], []
    for s in range(slots):
        m_low = hit(low, in_low, s)
        m_high = hit(high, in_high, s)
        low_rows.append(at(m_low, run_in))
        high_rows.append(at(m_high, run_in))
        run_in = run_in + m_low + m_high

    def top(x):
        return jnp.max(jnp.max(x, axis=0, keepdims=True), axis=1, keepdims=True)

    most, most_early = top(count), top(early)
    level = jnp.full((1, 1), float(len(plan.levels) - 1), jnp.float32)
    for i in range(len(plan.levels) - 2, -1, -1):
        wide, soon = plan.levels[i]
        level = jnp.where((most <= wide) & (most_early <= soon), float(i), level)

    lane = lax.broadcasted_iota(jnp.int32, (1, nrows), 1)
    e_send = lax.broadcasted_iota(jnp.int32, (plan.n_send, nrows), 0)
    e_fwd = lax.broadcasted_iota(jnp.int32, (plan.n_fwd, nrows), 0)
    e_loc = lax.broadcasted_iota(jnp.int32, (plan.n_loc, nrows), 0)
    t_send = jnp.zeros((plan.n_send, nrows), jnp.int32)
    t_fwd = jnp.zeros((plan.n_fwd, nrows), jnp.int32)
    t_loc = jnp.zeros((plan.n_loc, nrows), jnp.int32)
    mine = lane == me

    def put(table, index, where_, value, on):
        return table + jnp.where(index == jnp.where(on, where_, -1), value, 0)

    for s in range(slots):
        lo, hi = row(low, s), row(high, s)
        il, ih = row(in_low, s) == 1, row(in_high, s) == 1
        bo, si = row(both, s) == 1, row(single, s) == 1
        p_low = low_rows[s].astype(jnp.int32)
        p_high = high_rows[s].astype(jnp.int32)
        p_far = pos_rows[s].astype(jnp.int32)
        land = jnp.where(bo, land_rows[s], row(goal, s))
        other = lo + hi - land
        k_land = (land ^ lane) * cap + p_far
        value = jnp.full((1, nrows), s, jnp.int32)
        t_send = put(t_send, e_send, (lo ^ lane) * cap + p_low, value, il & mine)
        t_send = put(t_send, e_send, (hi ^ lane) * cap + p_high, value, ih & mine)
        t_send = put(t_send, e_send, k_land, value, (bo | si) & mine)
        part = row(pair_part, s)
        t_fwd = put(t_fwd, e_fwd, ((land ^ other) - 1) * plan.fwd + part, k_land, bo & (land == me))
        near = ((lane ^ me) & half) == 0
        lo_me = lo == me
        hi_me = hi == me
        ok = row(flag(live), s) == 1
        code_near = (lane ^ me) * cap + jnp.where(lo_me, p_low, p_high)
        code_fwd = plan.at_fwd + ((land ^ me) - 1) * plan.fwd + part
        code_far = jnp.where(bo & (land != me), code_fwd, k_land)
        code = jnp.where(near, code_near, code_far)
        a, b = row(first, s), row(second, s)
        t_loc = put(t_loc, e_loc, row(w_low, s) * NT + b, code, ok & lo_me)
        t_loc = put(t_loc, e_loc, row(w_high, s) * NT + a, code, ok & hi_me & (a != b))

    def column(table):
        return jnp.sum(table.astype(jnp.float32), axis=1, keepdims=True)

    wide_lane = out_ref.shape[1]

    def spread(table, start):
        col = column(table)
        shape = (col.shape[0], wide_lane)
        down = lax.broadcasted_iota(jnp.int32, shape, 0) + start
        across = lax.broadcasted_iota(jnp.int32, shape, 1)
        return jnp.sum(jnp.where(down == across, col, 0.0), axis=0, keepdims=True)

    line = spread(t_send, 0) + spread(t_fwd, plan.at_fwd) + spread(t_loc, plan.at_loc)
    across = lax.broadcasted_iota(jnp.int32, (1, wide_lane), 1)
    line = jnp.where(across == plan.at_level, level, line)
    out_ref[...] = line.astype(jnp.int32)


def route(plan, old_blocks, old_counts, new_phase):
    nrows, slots = old_blocks.shape
    wide = -(-(plan.at_level + 1) // LANES) * LANES
    return pl.pallas_call(
        functools.partial(route_kernel, plan, slots),
        out_shape=jax.ShapeDtypeStruct((1, wide), jnp.int32),
        in_specs=[
            pl.BlockSpec(memory_space=pltpu.VMEM),
            pl.BlockSpec(memory_space=pltpu.VMEM),
            pl.BlockSpec(memory_space=pltpu.SMEM),
        ],
        out_specs=pl.BlockSpec(memory_space=pltpu.VMEM),
        name="route",
    )(old_blocks.T, old_counts.reshape(1, nrows), new_phase)


def pack_kernel(streams, slots_pad, parts, table_ref, *refs):
    rows = refs[0].shape[0]
    flats = [ref.reshape(rows * slots_pad, LANES) for ref in refs[:parts]]
    f_refs, outs = refs[parts:-len(streams)], refs[-len(streams) :]
    for (base, count, carries), out in zip(streams, outs):

        def one(j, carry, base=base, out=out):
            slot = table_ref[0, base + j]
            for h, flat in enumerate(flats):
                for r in range(0, rows, 8):
                    n = min(8, rows - r)
                    piece = flat[pl.ds(r * slots_pad + slot, n, stride=slots_pad), :]
                    out[pl.ds(j * rows * parts + h * rows + r, n), :] = piece
            return carry

        lax.fori_loop(0, count, one, 0)
        if carries:
            (f_ref,) = f_refs
            mine, wide = f_ref.shape
            for h in range(wide // LANES):
                at = count * rows * parts + h * mine
                out[pl.ds(at, mine), :] = f_ref[:, h * LANES : (h + 1) * LANES]


def fock_rows(f_mine):
    return -(-f_mine.shape[0] * (f_mine.shape[1] // LANES) // 8) * 8


def pack(table, amp, f_mine, streams):
    rows, slots, occ = amp.shape
    parts = occ // LANES
    pad = -(-slots // 8) * 8
    extra = fock_rows(f_mine)
    shapes = [(n * rows * parts + (extra if c else 0), LANES) for _, n, c in streams]
    f_args = [f_mine] if any(c for _, _, c in streams) else []
    return pl.pallas_call(
        functools.partial(pack_kernel, streams, pad, parts),
        out_shape=[jax.ShapeDtypeStruct(shape, jnp.float32) for shape in shapes],
        in_specs=[
            pl.BlockSpec(memory_space=pltpu.SMEM),
            *[pl.BlockSpec((rows, pad, LANES), lambda i, h=h: (0, 0, h)) for h in range(parts)],
            *[pl.BlockSpec(x.shape, lambda i: (0, 0)) for x in f_args],
        ],
        out_specs=[pl.BlockSpec(shape, lambda i: (0, 0)) for shape in shapes],
        grid=(1,),
        compiler_params=pltpu.CompilerParams(vmem_limit_bytes=VMEM_LIMIT),
        name="pack",
    )(table, *[amp] * parts, *f_args)


def forward_kernel(plan, soon, size, table_ref, *refs):
    ins, outs = refs[: plan.half], refs[plan.half :]
    for k, out in enumerate(outs):

        def one(j, carry, k=k, out=out):
            code = table_ref[0, plan.at_fwd + k * plan.fwd + j]
            for f in range(plan.half):
                start = (plan.half + f) * plan.cap

                @pl.when((code >= start) & (code < start + soon))
                def _(f=f, start=start):
                    to, of = pl.multiple_of(j * size, 8), pl.multiple_of((code - start) * size, 8)
                    out[pl.ds(to, size), :] = ins[f][pl.ds(of, size), :]

            return carry

        lax.fori_loop(0, plan.fwd, one, 0)


def forward(plan, table, landed, soon, size):
    return pl.pallas_call(
        functools.partial(forward_kernel, plan, soon, size),
        out_shape=[jax.ShapeDtypeStruct((plan.fwd * size, LANES), jnp.float32)]
        * (plan.half - 1),
        in_specs=[pl.BlockSpec(memory_space=pltpu.SMEM)]
        + [pl.BlockSpec(memory_space=pltpu.VMEM)] * plan.half,
        out_specs=[pl.BlockSpec(memory_space=pltpu.VMEM)] * (plan.half - 1),
        compiler_params=pltpu.CompilerParams(vmem_limit_bytes=VMEM_LIMIT),
        name="forward",
    )(table, *landed)


def split(x):
    high = x.astype(jnp.bfloat16)
    return high, (x - high.astype(jnp.float32)).astype(jnp.bfloat16)


def contract_kernel(plan, tile, parts, pieces, f_piece, table_ref, phase_ref, *refs):
    n = len(pieces)
    ins, out_ref, blocks, dense, f_raw, f_hi, f_lo, sems = refs[:n], *refs[n:]
    step = pl.program_id(0)
    rows = tile * tile
    size = rows * parts
    me = lax.axis_index("row")
    mine, extra = f_piece

    @pl.when(step == 0)
    def _():
        copies = []
        for i, (ref, (start, count, sender)) in enumerate(zip(ins, pieces)):
            got = blocks.at[pl.ds(start * size, count * size)]
            copies.append(pltpu.make_async_copy(ref.at[pl.ds(0, count * size)], got, sems.at[0, i]))
            if sender is not None:
                got = f_raw.at[me ^ sender]
                part = ref.at[pl.ds(count * size, extra)]
                copies.append(pltpu.make_async_copy(part, got, sems.at[1, i]))
        for copy in copies:
            copy.start()
        for copy in copies:
            copy.wait()
        for device in range(plan.nrows):
            for h in range(f_hi.shape[1] // LANES):
                high, low = split(f_raw[device, h * mine : (h + 1) * mine, :])
                at = pl.ds(device * mine, mine), pl.ds(h * LANES, LANES)
                f_hi[at] = high
                f_lo[at] = low

    within = step // tile
    b = step - within * tile
    column = ((me - phase_ref[0]) & (plan.nrows - 1)) + within * plan.nrows
    b_global = column * tile + b
    sub = lax.broadcasted_iota(jnp.int32, (8, LANES), 0)
    for a in range(NT):
        code = table_ref[0, plan.at_loc + within * NT + a]
        for h in range(parts):
            base = code * size + h * rows
            for r in range(0, 16, 8):
                c_global = a * tile + r + sub
                left = blocks[pl.ds(base + b + r * tile, 8, stride=tile), :]
                right = blocks[pl.ds(base + b * tile + r, 8), :]
                value = jnp.where(
                    c_global < b_global, left, jnp.where(c_global > b_global, -right, 0.0)
                )
                if r + 8 > tile:
                    value = jnp.where(sub < tile - r, value, 0.0)
                dense[pl.ds(a * 16 + r, 8), pl.ds(h * LANES, LANES)] = value
    hi, lo = split(dense[...])
    dot = functools.partial(jnp.dot, preferred_element_type=jnp.float32)
    out_ref[0, 0] = dot(f_hi[...], hi) + (dot(f_lo[...], hi) + dot(f_hi[...], lo))


def contract(plan, table, new_phase, buffers, f_piece, tile, occ):
    parts = occ // LANES
    size = tile * tile * parts
    total = plan.n_send + plan.n_fwd
    width = plan.nrows * f_piece[0]
    pieces = tuple(buffer[:3] for buffer in buffers)
    return pl.pallas_call(
        functools.partial(contract_kernel, plan, tile, parts, pieces, f_piece),
        grid=(plan.per * tile,),
        out_shape=jax.ShapeDtypeStruct((plan.per, tile, width, occ), jnp.float32),
        in_specs=[pl.BlockSpec(memory_space=pltpu.SMEM)] * 2
        + [pl.BlockSpec(memory_space=pl.ANY)] * len(buffers),
        out_specs=pl.BlockSpec((1, 1, width, occ), lambda i: (i // tile, i % tile, 0, 0)),
        scratch_shapes=[
            pltpu.VMEM((total * size + 16 * tile, LANES), jnp.float32),
            pltpu.VMEM((NT * 16, occ), jnp.float32),
            pltpu.VMEM((plan.nrows, f_piece[1], LANES), jnp.float32),
            pltpu.VMEM((width, NT * 16), jnp.bfloat16),
            pltpu.VMEM((width, NT * 16), jnp.bfloat16),
            pltpu.SemaphoreType.DMA((2, len(buffers))),
        ],
        compiler_params=pltpu.CompilerParams(
            dimension_semantics=("arbitrary",), vmem_limit_bytes=VMEM_LIMIT
        ),
        name="contract",
    )(table, new_phase, *[buffer[3] for buffer in buffers])


def body(amplitudes, old_blocks, old_counts, new_phase, fock):
    nrows = lax.axis_size("row")
    slots, tile, _, occ = amplitudes.shape
    plan = Plan(nrows, slots)
    half, cap = plan.half, plan.cap
    size = tile * tile * occ // LANES

    def send(x, k):
        return lax.ppermute(x, "row", [(i, i ^ k) for i in range(nrows)])

    table = route(plan, old_blocks, old_counts, new_phase)
    mine = fock.shape[0]
    f_mine = jnp.pad(fock.reshape(mine, NT, tile), ((0, 0), (0, 0), (0, 16 - tile)))
    f_mine = f_mine.reshape(mine, NT * 16)
    f_piece = mine, fock_rows(f_mine)
    amp = jnp.transpose(amplitudes, (1, 2, 0, 3)).reshape(tile * tile, slots, occ)

    def branch(wide, soon, table, amp, new_phase, f_mine):
        late = wide - soon
        far = range(half, nrows)
        head = pack(table, amp, f_mine, [(k * cap, soon, not late) for k in far])
        landed = [send(head[k - half], k) for k in far]
        rest = [(k * cap, cap, True) for k in range(half)]
        rest += [(k * cap + soon, late, True) for k in far] if late else []
        rest = pack(table, amp, f_mine, rest)
        near_in = [rest[0]] + [send(rest[k], k) for k in range(1, half)]
        late_in = [send(rest[k], k) for k in far] if late else []
        relay = forward(plan, table, landed, soon, size)
        relay_in = [send(x, k + 1) for k, x in enumerate(relay)]
        buffers = [(k * cap, cap, k, near_in[k]) for k in range(half)]
        buffers += [(k * cap, soon, None if late else k, landed[k - half]) for k in far]
        buffers += [(k * cap + soon, late, k, late_in[k - half]) for k in far if late]
        buffers += [(plan.at_fwd + k * plan.fwd, plan.fwd, None, x) for k, x in enumerate(relay_in)]
        return contract(plan, table, new_phase, buffers, f_piece, tile, occ)

    return lax.switch(
        table[0, plan.at_level],
        [functools.partial(branch, *level) for level in plan.levels],
        table,
        amp,
        new_phase,
        f_mine,
    )


def solution(mesh):
    return jax.shard_map(
        body,
        mesh=mesh,
        in_specs=(P("row", None, None, "col"), P(), P(), P(), P("row", None)),
        out_specs=P("row", None, None, "col"),
        check_vma=False,
    )
```

time: 240 us -> 162 us (0.68)
  blocking collectives: 163 us -> 0 us
  waiting for transfers between devices: 0.01 us -> 88 us
  matrix products: 27.7 us -> 0 us
  Pallas kernels: 0 us -> 26.7 us
  starting transfers between devices: 13.4 us -> 37.4 us
  local copies, waits for them, and re-layouts: 27 us -> 8.33 us
  other arithmetic: 6.61 us -> 0 us
    all_gather x1 -> x0, blocking collectives: 163 us -> none  [body(): fock_full = lax.all_gather(fock, 'row', axis=0, tiled=True)]
    ppermute x0 -> x14, waiting for transfers between devices: none -> 88 us  [send(): return lax.ppermute(x, 'row', [(i, i ^ k) for i in range(nrows)])]
    ppermute x0 -> x14, starting transfers between devices: none -> 37.4 us  [send(): return lax.ppermute(x, 'row', [(i, i ^ k) for i in range(nrows)])]
    dot_general x5 -> x0, matrix products: 27.7 us -> none  [the longest x2 18.3 us: body(): chosen = jnp.dot(picker, received, precision=lax.Precision.HIGHEST)]
    pallas_call x0 -> x5, Pallas kernels: none -> 26.7 us  [the longest x2 11.4 us: pack(): pl.pallas_call(functools.partial(pack_kernel, streams, pad, parts), out_s...]
    all_to_all x2 -> x0, starting transfers between devices: 13.4 us -> none  [the longest x1 7.28 us: body(): lax.all_to_all(sent_ids, 'row', split_axis=0, concat_axis=0, tiled=True)]
    dot_general x1 -> x0, local copies, waits for them, and re-layouts: 8.85 us -> none  [body(): chosen = jnp.dot(picker, received, precision=lax.Precision.HIGHEST)]
    reshape x3 -> x2, local copies, waits for them, and re-layouts: 5.81 us -> 1.51 us  [the longest x1 0.79 us: body(): fock.reshape(mine, NT, tile)]
  transfers between devices with their start and end apart: 2 -> 14, of which waited for: 0 -> 8; matrix products, arithmetic and copies ran while one was open for 6% -> 2% of each run, Pallas kernels for 0% -> 6%
where the time goes in v1:
time: 162 us
  waiting for transfers between devices  88 us (54%)
  starting transfers between devices  37.4 us (23%)
  Pallas kernels  26.7 us (16%)
  local copies, waits for them, and re-layouts  8.33 us (5%)
    ppermute x14, waiting for transfers between devices, send(): return lax.ppermute(x, 'row', [(i, i ^ k) for i in range(nrows)])  88 us
    ppermute x14, starting transfers between devices, send(): return lax.ppermute(x, 'row', [(i, i ^ k) for i in range(nrows)])  37.4 us
    pallas_call x2, Pallas kernels, pack(): pl.pallas_call(functools.partial(pack_kernel, streams, pad, parts), out_s...  11.4 us
    pallas_call x1, Pallas kernels, contract(): pl.pallas_call(functools.partial(contract_kernel, plan, tile, parts, piec...  10.6 us
  transfers between devices with their start and end apart: 14, of which 8 were waited for; matrix products, arithmetic and copies ran while one was open for 2% of the time, Pallas kernels for 6%

profile of v1, /device:TPU:0, one launch (start us, length us, event | category | flops | bytes accessed | tf_op | source)
XLA Modules:
  0.0 162.0 jit_solution(5338201213387165520)
XLA Ops:
  0.7 1.4 copy.13
  2.0 1.8 %route.1 = s32[1,128]{1,0:T(1,128)S(1)} custom-call(s32[25,8]{1,0:T(8,128)} %bitcast.22, s32[1,8]{1,0:T(1,128)} %bitcast.23, s32[1]{0:T(128)S(6)} %copy.17.phase_ref), custom_call_target="tpu_custom_call" | custom-call | tf_op jit(solution)/shard_map/route/pallas_call | solution.py:180
  3.9 0.6 slice.3
  5.1 155.2 %conditional.1 = (f32[2,10,160,256]{3,2,1,0:T(8,128)S(1)}) conditional(s32[]{:T(128)} %bitcast.5, (s32[1,128]{1,0:T(1,128)S(1)}, f32[10,10,25,256]{3,2,1,0:T(8,128)}, f32[20,160]{1,0:T(8,128)}, s32[1]{0:T(128)}, ()) %tuple.28, (s32[1,128]{1,0:T(1,128)S(1)}, f32[10,10,25,256]{3,2,1,0:T(8,128)}, f32[20,160]{1,0:T(8,128)}, s32[1]{0:T(128)}, ...), branch_computations={%region_0.1_spmd, %region_1.2_spmd, %region_2.3_spmd} | conditional | bytes 58151364 | solution.py:397
  5.1 0.0 copy-start.28
  5.1 0.0 copy-start
  5.1 5.0 %pack.7 = (f32[800,128]{1,0:T(8,128)}, f32[800,128]{1,0:T(8,128)}, f32[800,128]{1,0:T(8,128)}, f32[800,128]{1,0:T(8,128)}) custom-call(s32[1,128]{1,0:T(1,128)S(1)} %get-tuple-element.32.table_ref, f32[100,25,256]{2,1,0:T(8,128)} %bitcast.10, f32[100,25,256]{2,1,0:T(8,128)} %bitcast.11), custom_call_target="tpu_custom_call" | custom-call | tf_op jit(solution)/shard_map/cond/branch_0_fun/pack/pallas_call | solution.py:228
  10.1 4.1 %collective-permute-start.3 = (f32[800,128]{1,0:T(8,128)}, f32[800,128]{1,0:T(8,128)}, u32[]{:S(2)}, u32[]{:S(2)}) collective-permute-start(f32[800,128]{1,0:T(8,128)} %get-tuple-element.41), channel_id=1, source_target_pairs={{0,16},{4,20},{8,24},{12,28},{16,0},{20,4},{24,8},{28,12},{1,17},{... | collective-permute-start | bytes 1228808 | tf_op jit(solution)/shard_map/cond/branch_0_fun/ppermute | solution.py:370
  14.2 1.3 collective-permute-start.4
  15.5 3.6 %collective-permute-start.5 = (f32[800,128]{1,0:T(8,128)}, f32[800,128]{1,0:T(8,128)}, u32[]{:S(2)}, u32[]{:S(2)}) collective-permute-start(f32[800,128]{1,0:T(8,128)} %get-tuple-element.43), channel_id=1, source_target_pairs={{0,24},{4,28},{8,16},{12,20},{16,8},{20,12},{24,0},{28,4},{1,25},{... | collective-permute-start | bytes 1228808 | tf_op jit(solution)/shard_map/cond/branch_0_fun/ppermute | solution.py:370
  19.1 0.0 collective-permute-start.6
  19.1 0.0 copy-done.28
  19.1 0.8 reshape.25
  19.9 0.9 pad.5
  20.8 0.7 reshape.22.refs_2_
  21.5 6.4 %pack.6 = (f32[1640,128]{1,0:T(8,128)}, f32[1640,128]{1,0:T(8,128)}, f32[1640,128]{1,0:T(8,128)}, f32[1640,128]{1,0:T(8,128)}, f32[240,128]{1,0:T(8,128)}, /*ind...) custom-call(s32[1,128]{1,0:T(1,128)S(1)} %get-tuple-element.32.table_ref, f32[100,25,256]{2,1,0:T(8,128)S(1)} %bitcast.12, ...), custom_call_target="tpu_custom_call" | custom-call | tf_op jit(solution)/shard_map/cond/branch_0_fun/pack/pallas_call | solution.py:228
  27.9 1.0 collective-permute-start.7
  28.9 33.7 %collective-permute-done.3.refs_0_.refs_4_ = f32[800,128]{1,0:T(8,128)} collective-permute-done((f32[800,128]{1,0:T(8,128)}, f32[800,128]{1,0:T(8,128)}, u32[]{:S(2)}, u32[]{:S(2)}) %collective-permute-start.3) | collective-permute-done | bytes 409632 | tf_op jit(solution)/shard_map/cond/branch_0_fun/ppermute | solution.py:370
  62.6 1.8 %collective-permute-start = (f32[1640,128]{1,0:T(8,128)}, f32[1640,128]{1,0:T(8,128)S(1)}, u32[]{:S(2)}, u32[]{:S(2)}) collective-permute-start(f32[1640,128]{1,0:T(8,128)} %get-tuple-element.38), channel_id=1, source_target_pairs={{0,4},{4,0},{8,12},{12,8},{16,20},{20,16},{24,28},{28,24},{1,5},{5... | collective-permute-start | bytes 2519048 | tf_op jit(solution)/shard_map/cond/branch_0_fun/ppermute | solution.py:370
  64.4 8.2 %collective-permute-done.4.refs_1_.refs_5_ = f32[800,128]{1,0:T(8,128)} collective-permute-done((f32[800,128]{1,0:T(8,128)}, f32[800,128]{1,0:T(8,128)}, u32[]{:S(2)}, u32[]{:S(2)}) %collective-permute-start.4) | collective-permute-done | bytes 409632 | tf_op jit(solution)/shard_map/cond/branch_0_fun/ppermute | solution.py:370
  72.6 0.0 collective-permute-start.1
  72.6 0.0 collective-permute-done.5.refs_2_.refs_6_
  72.6 9.3 %collective-permute-start.2 = (f32[1640,128]{1,0:T(8,128)}, f32[1640,128]{1,0:T(8,128)S(1)}, u32[]{:S(2)}, u32[]{:S(2)}) collective-permute-start(f32[1640,128]{1,0:T(8,128)} %get-tuple-element.40), channel_id=1, source_target_pairs={{0,12},{4,8},{8,4},{12,0},{16,28},{20,24},{24,20},{28,16},{1,13},{... | collective-permute-start | bytes 2519048 | tf_op jit(solution)/shard_map/cond/branch_0_fun/ppermute | solution.py:370
  81.9 0.0 collective-permute-done.6.refs_3_.refs_7_
  81.9 2.9 %forward.3 = (f32[800,128]{1,0:T(8,128)}, f32[800,128]{1,0:T(8,128)}, f32[800,128]{1,0:T(8,128)}) custom-call(s32[1,128]{1,0:T(1,128)S(1)} %get-tuple-element.32.table_ref, f32[800,128]{1,0:T(8,128)} %collective-permute-done.3.refs_0_.refs_4_, f32[800,128]{1,0:T(8,128)} %collective-permute-done.4.refs_1_.refs_5_, ...), custom_call_target="tpu_custom_call" | custom-call | tf_op jit(solution)/shard_map/cond/branch_0_fun/forward/pallas_call | solution.py:263
  84.8 0.2 collective-permute-start.11
  85.0 5.7 %collective-permute-done.7.refs_8_ = f32[240,128]{1,0:T(8,128)S(1)} collective-permute-done((f32[240,128]{1,0:T(8,128)}, f32[240,128]{1,0:T(8,128)S(1)}, u32[]{:S(2)}, u32[]{:S(2)}) %collective-permute-start.7) | collective-permute-done | bytes 122912 | tf_op jit(solution)/shard_map/cond/branch_0_fun/ppermute | solution.py:370
  90.7 5.3 %collective-permute-start.8 = (f32[240,128]{1,0:T(8,128)}, f32[240,128]{1,0:T(8,128)S(1)}, u32[]{:S(2)}, u32[]{:S(2)}) collective-permute-start(f32[240,128]{1,0:T(8,128)} %get-tuple-element.46), channel_id=1, source_target_pairs={{0,20},{4,16},{8,28},{12,24},{16,4},{20,0},{24,12},{28,8},{1,21},{... | collective-permute-start | bytes 368648 | tf_op jit(solution)/shard_map/cond/branch_0_fun/ppermute | solution.py:370
  96.1 14.2 %collective-permute-done.8.refs_9_ = f32[240,128]{1,0:T(8,128)S(1)} collective-permute-done((f32[240,128]{1,0:T(8,128)}, f32[240,128]{1,0:T(8,128)S(1)}, u32[]{:S(2)}, u32[]{:S(2)}) %collective-permute-start.8) | collective-permute-done | bytes 122912 | tf_op jit(solution)/shard_map/cond/branch_0_fun/ppermute | solution.py:370
  110.3 5.4 %collective-permute-start.9 = (f32[240,128]{1,0:T(8,128)}, f32[240,128]{1,0:T(8,128)S(1)}, u32[]{:S(2)}, u32[]{:S(2)}) collective-permute-start(f32[240,128]{1,0:T(8,128)} %get-tuple-element.47), channel_id=1, source_target_pairs={{0,24},{4,28},{8,16},{12,20},{16,8},{20,12},{24,0},{28,4},{1,25},{... | collective-permute-start | bytes 368648 | tf_op jit(solution)/shard_map/cond/branch_0_fun/ppermute | solution.py:370
  115.7 3.1 %collective-permute-done.9.refs_10_ = f32[240,128]{1,0:T(8,128)S(1)} collective-permute-done((f32[240,128]{1,0:T(8,128)}, f32[240,128]{1,0:T(8,128)S(1)}, u32[]{:S(2)}, u32[]{:S(2)}) %collective-permute-start.9) | collective-permute-done | bytes 122912 | tf_op jit(solution)/shard_map/cond/branch_0_fun/ppermute | solution.py:370
  118.8 2.5 %collective-permute-start.10 = (f32[240,128]{1,0:T(8,128)}, f32[240,128]{1,0:T(8,128)S(1)}, u32[]{:S(2)}, u32[]{:S(2)}) collective-permute-start(f32[240,128]{1,0:T(8,128)} %get-tuple-element.48), channel_id=1, source_target_pairs={{0,28},{4,24},{8,20},{12,16},{16,12},{20,8},{24,4},{28,0},{1,29},{... | collective-permute-start | bytes 368648 | tf_op jit(solution)/shard_map/cond/branch_0_fun/ppermute | solution.py:370
  121.3 5.4 %collective-permute-done.10.refs_11_ = f32[240,128]{1,0:T(8,128)S(1)} collective-permute-done((f32[240,128]{1,0:T(8,128)}, f32[240,128]{1,0:T(8,128)S(1)}, u32[]{:S(2)}, u32[]{:S(2)}) %collective-permute-start.10) | collective-permute-done | bytes 122912 | tf_op jit(solution)/shard_map/cond/branch_0_fun/ppermute | solution.py:370
  126.7 0.0 copy-done.30
  126.7 0.6 copy-done.33
  127.4 2.9 %collective-permute-start.12 = (f32[800,128]{1,0:T(8,128)}, f32[800,128]{1,0:T(8,128)S(1)}, u32[]{:S(2)}, u32[]{:S(2)}) collective-permute-start(f32[800,128]{1,0:T(8,128)} %get-tuple-element.50), channel_id=1, source_target_pairs={{0,8},{4,12},{8,0},{12,4},{16,24},{20,28},{24,16},{28,20},{1,9},{5... | collective-permute-start | bytes 1228808 | tf_op jit(solution)/shard_map/cond/branch_0_fun/ppermute | solution.py:370
  130.2 0.0 collective-permute-done.11.refs_12_
  130.2 0.0 collective-permute-start.13
  130.3 10.5 %collective-permute-done.12.refs_13_ = f32[800,128]{1,0:T(8,128)S(1)} collective-permute-done((f32[800,128]{1,0:T(8,128)}, f32[800,128]{1,0:T(8,128)S(1)}, u32[]{:S(2)}, u32[]{:S(2)}) %collective-permute-start.12) | collective-permute-done | bytes 409632 | tf_op jit(solution)/shard_map/cond/branch_0_fun/ppermute | solution.py:370
  140.8 7.3 %collective-permute-done.13.refs_14_ = f32[800,128]{1,0:T(8,128)S(1)} collective-permute-done((f32[800,128]{1,0:T(8,128)}, f32[800,128]{1,0:T(8,128)S(1)}, u32[]{:S(2)}, u32[]{:S(2)}) %collective-permute-start.13) | collective-permute-done | bytes 409632 | tf_op jit(solution)/shard_map/cond/branch_0_fun/ppermute | solution.py:370
  148.0 0.0 collective-permute-done.refs_1_
  148.0 0.0 collective-permute-done.1.refs_2_
  148.0 0.0 collective-permute-done.2.refs_3_
  148.1 1.3 copy-done.20
  149.4 0.2 copy-done.7
  149.6 10.6 %contract.3 = f32[2,10,160,256]{3,2,1,0:T(8,128)S(1)} custom-call(s32[1,128]{1,0:T(1,128)S(1)} %get-tuple-element.32.table_ref, s32[1]{0:T(128)} %get-tuple-element.34.phase_ref, f32[1640,128]{1,0:T(8,128)} %get-tuple-element.37.refs_0_, f32[1640,128]{1,0:T(8,128)} %copy-done.7, f32[1640,128]{1,0:T(8,128)} %copy-done.8, f32[1640,128]{1,0:T(8,128)} %copy-done.9, ...), custom_call_target="tpu_custom_call" | custom-call | tf_op jit(solution)/shard_map/cond/branch_0_fun/contract/pallas_call | solution.py:340
  160.3 0.0 copy-start.3
  160.3 1.7 %copy-done.3 = f32[2,10,160,256]{3,2,1,0:T(8,128)} copy-done((f32[2,10,160,256]{3,2,1,0:T(8,128)}, f32[2,10,160,256]{3,2,1,0:T(8,128)S(1)}, u32[]{:S(2)}) %copy-start.3) | copy-done | bytes 3276824
  (17 shorter events, 0.0 us)
Async XLA Ops:
  5.1 13.9 %copy-start.28 = (f32[20,160]{1,0:T(8,128)S(1)}, f32[20,160]{1,0:T(8,128)}, u32[]{:S(2)}) copy-start(f32[20,160]{1,0:T(8,128)} %get-tuple-element.105) | copy-start | bytes 38404 | tf_op jit(solution)/shard_map/cond
  5.1 16.4 %copy-start = (f32[10,10,25,256]{3,2,1,0:T(8,128)S(1)}, f32[10,10,25,256]{3,2,1,0:T(8,128)}, u32[]{:S(2)}) copy-start(f32[10,10,25,256]{3,2,1,0:T(8,128)} %get-tuple-element.87) | copy-start | bytes 7680004 | tf_op jit(solution)/shard_map/cond
  10.1 52.4 %collective-permute-start.3 = (f32[800,128]{1,0:T(8,128)}, f32[800,128]{1,0:T(8,128)}, u32[]{:S(2)}, u32[]{:S(2)}) collective-permute-start(f32[800,128]{1,0:T(8,128)} %get-tuple-element.41), channel_id=1, source_target_pairs={{0,16},{4,20},{8,24},{12,28},{16,0},{20,4},{24,8},{28,12},{1,17},{... | collective-permute-start | bytes 1228808 | tf_op jit(solution)/shard_map/cond/branch_0_fun/ppermute | solution.py:370
  14.2 58.4 %collective-permute-start.4 = (f32[800,128]{1,0:T(8,128)}, f32[800,128]{1,0:T(8,128)}, u32[]{:S(2)}, u32[]{:S(2)}) collective-permute-start(f32[800,128]{1,0:T(8,128)} %get-tuple-element.42), channel_id=1, source_target_pairs={{0,20},{4,16},{8,28},{12,24},{16,4},{20,0},{24,12},{28,8},{1,21},{... | collective-permute-start | bytes 1228808 | tf_op jit(solution)/shard_map/cond/branch_0_fun/ppermute | solution.py:370
  15.5 57.1 %collective-permute-start.5 = (f32[800,128]{1,0:T(8,128)}, f32[800,128]{1,0:T(8,128)}, u32[]{:S(2)}, u32[]{:S(2)}) collective-permute-start(f32[800,128]{1,0:T(8,128)} %get-tuple-element.43), channel_id=1, source_target_pairs={{0,24},{4,28},{8,16},{12,20},{16,8},{20,12},{24,0},{28,4},{1,25},{... | collective-permute-start | bytes 1228808 | tf_op jit(solution)/shard_map/cond/branch_0_fun/ppermute | solution.py:370
  19.1 62.9 %collective-permute-start.6 = (f32[800,128]{1,0:T(8,128)}, f32[800,128]{1,0:T(8,128)}, u32[]{:S(2)}, u32[]{:S(2)}) collective-permute-start(f32[800,128]{1,0:T(8,128)} %get-tuple-element.44), channel_id=1, source_target_pairs={{0,28},{4,24},{8,20},{12,16},{16,12},{20,8},{24,4},{28,0},{1,29},{... | collective-permute-start | bytes 1228808 | tf_op jit(solution)/shard_map/cond/branch_0_fun/ppermute | solution.py:370
  27.9 62.8 %collective-permute-start.7 = (f32[240,128]{1,0:T(8,128)}, f32[240,128]{1,0:T(8,128)S(1)}, u32[]{:S(2)}, u32[]{:S(2)}) collective-permute-start(f32[240,128]{1,0:T(8,128)} %get-tuple-element.45), channel_id=1, source_target_pairs={{0,16},{4,20},{8,24},{12,28},{16,0},{20,4},{24,8},{28,12},{1,17},{... | collective-permute-start | bytes 368648 | tf_op jit(solution)/shard_map/cond/branch_0_fun/ppermute | solution.py:370
  62.6 85.5 %collective-permute-start = (f32[1640,128]{1,0:T(8,128)}, f32[1640,128]{1,0:T(8,128)S(1)}, u32[]{:S(2)}, u32[]{:S(2)}) collective-permute-start(f32[1640,128]{1,0:T(8,128)} %get-tuple-element.38), channel_id=1, source_target_pairs={{0,4},{4,0},{8,12},{12,8},{16,20},{20,16},{24,28},{28,24},{1,5},{5... | collective-permute-start | bytes 2519048 | tf_op jit(solution)/shard_map/cond/branch_0_fun/ppermute | solution.py:370
  72.6 75.5 %collective-permute-start.1 = (f32[1640,128]{1,0:T(8,128)}, f32[1640,128]{1,0:T(8,128)S(1)}, u32[]{:S(2)}, u32[]{:S(2)}) collective-permute-start(f32[1640,128]{1,0:T(8,128)} %get-tuple-element.39), channel_id=1, source_target_pairs={{0,8},{4,12},{8,0},{12,4},{16,24},{20,28},{24,16},{28,20},{1,9},{5... | collective-permute-start | bytes 2519048 | tf_op jit(solution)/shard_map/cond/branch_0_fun/ppermute | solution.py:370
  72.6 75.5 %collective-permute-start.2 = (f32[1640,128]{1,0:T(8,128)}, f32[1640,128]{1,0:T(8,128)S(1)}, u32[]{:S(2)}, u32[]{:S(2)}) collective-permute-start(f32[1640,128]{1,0:T(8,128)} %get-tuple-element.40), channel_id=1, source_target_pairs={{0,12},{4,8},{8,4},{12,0},{16,28},{20,24},{24,20},{28,16},{1,13},{... | collective-permute-start | bytes 2519048 | tf_op jit(solution)/shard_map/cond/branch_0_fun/ppermute | solution.py:370
  84.8 45.4 %collective-permute-start.11 = (f32[800,128]{1,0:T(8,128)}, f32[800,128]{1,0:T(8,128)S(1)}, u32[]{:S(2)}, u32[]{:S(2)}) collective-permute-start(f32[800,128]{1,0:T(8,128)} %get-tuple-element.49), channel_id=1, source_target_pairs={{0,4},{4,0},{8,12},{12,8},{16,20},{20,16},{24,28},{28,24},{1,5},{5... | collective-permute-start | bytes 1228808 | tf_op jit(solution)/shard_map/cond/branch_0_fun/ppermute | solution.py:370
  90.7 36.0 %copy-start.30 = (f32[240,128]{1,0:T(8,128)}, f32[240,128]{1,0:T(8,128)S(1)}, u32[]{:S(2)}) copy-start(f32[240,128]{1,0:T(8,128)S(1)} %collective-permute-done.7.refs_8_) | copy-start | bytes 368644 | tf_op jit(solution)/shard_map/cond
  90.7 19.6 %collective-permute-start.8 = (f32[240,128]{1,0:T(8,128)}, f32[240,128]{1,0:T(8,128)S(1)}, u32[]{:S(2)}, u32[]{:S(2)}) collective-permute-start(f32[240,128]{1,0:T(8,128)} %get-tuple-element.46), channel_id=1, source_target_pairs={{0,20},{4,16},{8,28},{12,24},{16,4},{20,0},{24,12},{28,8},{1,21},{... | collective-permute-start | bytes 368648 | tf_op jit(solution)/shard_map/cond/branch_0_fun/ppermute | solution.py:370
  110.3 16.4 %copy-start.31 = (f32[240,128]{1,0:T(8,128)}, f32[240,128]{1,0:T(8,128)S(1)}, u32[]{:S(2)}) copy-start(f32[240,128]{1,0:T(8,128)S(1)} %collective-permute-done.8.refs_9_) | copy-start | bytes 368644 | tf_op jit(solution)/shard_map/cond
  110.3 8.5 %collective-permute-start.9 = (f32[240,128]{1,0:T(8,128)}, f32[240,128]{1,0:T(8,128)S(1)}, u32[]{:S(2)}, u32[]{:S(2)}) collective-permute-start(f32[240,128]{1,0:T(8,128)} %get-tuple-element.47), channel_id=1, source_target_pairs={{0,24},{4,28},{8,16},{12,20},{16,8},{20,12},{24,0},{28,4},{1,25},{... | collective-permute-start | bytes 368648 | tf_op jit(solution)/shard_map/cond/branch_0_fun/ppermute | solution.py:370
  118.8 7.9 %copy-start.32 = (f32[240,128]{1,0:T(8,128)}, f32[240,128]{1,0:T(8,128)S(1)}, u32[]{:S(2)}) copy-start(f32[240,128]{1,0:T(8,128)S(1)} %collective-permute-done.9.refs_10_) | copy-start | bytes 368644 | tf_op jit(solution)/shard_map/cond
  118.8 7.9 %collective-permute-start.10 = (f32[240,128]{1,0:T(8,128)}, f32[240,128]{1,0:T(8,128)S(1)}, u32[]{:S(2)}, u32[]{:S(2)}) collective-permute-start(f32[240,128]{1,0:T(8,128)} %get-tuple-element.48), channel_id=1, source_target_pairs={{0,28},{4,24},{8,20},{12,16},{16,12},{20,8},{24,4},{28,0},{1,29},{... | collective-permute-start | bytes 368648 | tf_op jit(solution)/shard_map/cond/branch_0_fun/ppermute | solution.py:370
  126.7 0.7 copy-start.33
  127.4 13.4 %collective-permute-start.12 = (f32[800,128]{1,0:T(8,128)}, f32[800,128]{1,0:T(8,128)S(1)}, u32[]{:S(2)}, u32[]{:S(2)}) collective-permute-start(f32[800,128]{1,0:T(8,128)} %get-tuple-element.50), channel_id=1, source_target_pairs={{0,8},{4,12},{8,0},{12,4},{16,24},{20,28},{24,16},{28,20},{1,9},{5... | collective-permute-start | bytes 1228808 | tf_op jit(solution)/shard_map/cond/branch_0_fun/ppermute | solution.py:370
  130.2 17.8 %copy-start.16 = (f32[800,128]{1,0:T(8,128)}, f32[800,128]{1,0:T(8,128)S(1)}, u32[]{:S(2)}) copy-start(f32[800,128]{1,0:T(8,128)S(1)} %collective-permute-done.11.refs_12_) | copy-start | bytes 1228804 | tf_op jit(solution)/shard_map/cond
  130.2 17.8 %collective-permute-start.13 = (f32[800,128]{1,0:T(8,128)}, f32[800,128]{1,0:T(8,128)S(1)}, u32[]{:S(2)}, u32[]{:S(2)}) collective-permute-start(f32[800,128]{1,0:T(8,128)} %get-tuple-element.51), channel_id=1, source_target_pairs={{0,12},{4,8},{8,4},{12,0},{16,28},{20,24},{24,20},{28,16},{1,13},{... | collective-permute-start | bytes 1228808 | tf_op jit(solution)/shard_map/cond/branch_0_fun/ppermute | solution.py:370
  140.8 7.3 %copy-start.17 = (f32[800,128]{1,0:T(8,128)}, f32[800,128]{1,0:T(8,128)S(1)}, u32[]{:S(2)}) copy-start(f32[800,128]{1,0:T(8,128)S(1)} %collective-permute-done.12.refs_13_) | copy-start | bytes 1228804 | tf_op jit(solution)/shard_map/cond
  148.0 1.4 copy-start.20
  148.0 1.6 copy-start.7
  148.0 1.4 copy-start.8
  148.1 1.4 copy-start.9
  160.3 1.7 %copy-start.3 = (f32[2,10,160,256]{3,2,1,0:T(8,128)}, f32[2,10,160,256]{3,2,1,0:T(8,128)S(1)}, u32[]{:S(2)}) copy-start(f32[2,10,160,256]{3,2,1,0:T(8,128)S(1)} %get-tuple-element.111) | copy-start | bytes 9830404

commit v2 on v1

--- a/solution.py
+++ b/solution.py
@@ -17,6 +17,7 @@
     def __init__(self, nrows, slots):
         self.nrows = nrows
         self.half = nrows // 2
+        self.quarter = nrows // 4
         self.per = NT // nrows
         self.cap = self.per * ((slots - 2) // 8 + 2)
         self.fwd = self.per * self.per
@@ -27,9 +28,14 @@
         self.at_loc = self.n_send + self.n_fwd
         self.at_level = self.at_loc + self.n_loc
         cap = self.cap
-        wide = -(-5 * cap // 8), -(-6 * cap // 8), cap
-        early = -(-cap // 2), -(-cap // 2), cap
-        self.levels = tuple(zip(wide, early))
+        part = [-(-i * cap // 8) for i in range(9)]
+        levels = (
+            (part[5], part[3], part[6]),
+            (part[6], part[3], part[6]),
+            (part[6], part[4], cap),
+            (cap, cap, cap),
+        )
+        self.levels = tuple(dict.fromkeys(levels))
 
 
 def route_kernel(plan, slots, ids_ref, counts_ref, phase_ref, out_ref):
@@ -50,8 +56,6 @@
     w_low = lax.shift_right_logical(first, shift)
     w_high = lax.shift_right_logical(second, shift)
     pair_part = jnp.where(low < high, w_low * per + w_high, w_high * per + w_low)
-    far_low = ((low ^ src) & half) != 0
-    far_high = ((high ^ src) & half) != 0
     same = low == high
     one = jnp.int32(1)
     zero = jnp.int32(0)
@@ -59,14 +63,18 @@
     def flag(x):
         return jnp.where(x, one, zero)
 
-    in_low = flag(live & ~far_low)
-    in_high = flag(live & ~far_high & ~same)
-    x_low = flag(live & far_low)
-    x_high = flag(live & far_high & ~same)
-    both = x_low * x_high
-    single = x_low + x_high - 2 * both
-    goal = jnp.where(x_low == 1, low, high)
+    def group(owner):
+        away = owner ^ src
+        return jnp.where((away & half) != 0, 2, flag((away & plan.quarter) != 0))
+
+    g_low, g_high = group(low), group(high)
+    shared = flag(live & (g_low == g_high) & (g_low > 0) & ~same)
+    on_low = flag(live) * (1 - shared)
+    on_high = flag(live & ~same) * (1 - shared)
     dest = lax.broadcasted_iota(jnp.int32, (nrows, nrows), 0)
+    away = dest ^ lax.broadcasted_iota(jnp.int32, (nrows, nrows), 1)
+    is_far = (away & half) != 0
+    is_next = ~is_far & ((away & plan.quarter) != 0)
 
     def row(x, s):
         return x[s : s + 1, :]
@@ -78,16 +86,13 @@
         return jnp.sum(mask * run, axis=0, keepdims=True)
 
     count = jnp.zeros((nrows, nrows), jnp.float32)
-    singles = []
     for s in range(slots):
-        mask = hit(goal, single, s)
-        singles.append(mask)
-        count = count + mask
+        count = count + hit(low, on_low, s) + hit(high, on_high, s)
     early = jnp.zeros((nrows, nrows), jnp.float32)
-    land_rows, pos_rows = [], []
+    land_rows, pos_rows, low_rows, high_rows = [], [], [], []
     for s in range(slots):
-        m_low = hit(low, both, s)
-        m_high = hit(high, both, s)
+        m_low = hit(low, shared, s)
+        m_high = hit(high, shared, s)
         take = at(m_low, count) <= at(m_high, count)
         mask = jnp.where(take, m_low, m_high)
         pos_rows.append(at(mask, early))
@@ -96,25 +101,22 @@
         count = count + mask
     run = early
     for s in range(slots):
-        pos_rows[s] = pos_rows[s] + at(singles[s], run)
-        run = run + singles[s]
-    run_in = jnp.zeros((nrows, nrows), jnp.float32)
-    low_rows, high_rows = [], []
-    for s in range(slots):
-        m_low = hit(low, in_low, s)
-        m_high = hit(high, in_high, s)
-        low_rows.append(at(m_low, run_in))
-        high_rows.append(at(m_high, run_in))
-        run_in = run_in + m_low + m_high
+        m_low, m_high = hit(low, on_low, s), hit(high, on_high, s)
+        low_rows.append(at(m_low, run))
+        high_rows.append(at(m_high, run))
+        run = run + m_low + m_high
 
     def top(x):
         return jnp.max(jnp.max(x, axis=0, keepdims=True), axis=1, keepdims=True)
 
-    most, most_early = top(count), top(early)
+    most = top(jnp.where(is_far, count, 0.0))
+    most_early = top(jnp.where(is_far, early, 0.0))
+    most_next = top(jnp.where(is_next, count, 0.0))
     level = jnp.full((1, 1), float(len(plan.levels) - 1), jnp.float32)
     for i in range(len(plan.levels) - 2, -1, -1):
-        wide, soon = plan.levels[i]
-        level = jnp.where((most <= wide) & (most_early <= soon), float(i), level)
+        wide, soon, following = plan.levels[i]
+        fits = (most <= wide) & (most_early <= soon) & (most_next <= following)
+        level = jnp.where(fits, float(i), level)
 
     lane = lax.broadcasted_iota(jnp.int32, (1, nrows), 1)
     e_send = lax.broadcasted_iota(jnp.int32, (plan.n_send, nrows), 0)
@@ -129,30 +131,25 @@
         return table + jnp.where(index == jnp.where(on, where_, -1), value, 0)
 
     for s in range(slots):
-        lo, hi = row(low, s), row(high, s)
-        il, ih = row(in_low, s) == 1, row(in_high, s) == 1
-        bo, si = row(both, s) == 1, row(single, s) == 1
+        lo, hi, land = row(low, s), row(high, s), land_rows[s]
+        both = row(shared, s) == 1
         p_low = low_rows[s].astype(jnp.int32)
         p_high = high_rows[s].astype(jnp.int32)
-        p_far = pos_rows[s].astype(jnp.int32)
-        land = jnp.where(bo, land_rows[s], row(goal, s))
         other = lo + hi - land
-        k_land = (land ^ lane) * cap + p_far
+        k_low = (lo ^ lane) * cap + p_low
+        k_high = (hi ^ lane) * cap + p_high
+        k_land = (land ^ lane) * cap + pos_rows[s].astype(jnp.int32)
         value = jnp.full((1, nrows), s, jnp.int32)
-        t_send = put(t_send, e_send, (lo ^ lane) * cap + p_low, value, il & mine)
-        t_send = put(t_send, e_send, (hi ^ lane) * cap + p_high, value, ih & mine)
-        t_send = put(t_send, e_send, k_land, value, (bo | si) & mine)
+        t_send = put(t_send, e_send, k_low, value, (row(on_low, s) == 1) & mine)
+        t_send = put(t_send, e_send, k_high, value, (row(on_high, s) == 1) & mine)
+        t_send = put(t_send, e_send, k_land, value, both & mine)
         part = row(pair_part, s)
-        t_fwd = put(t_fwd, e_fwd, ((land ^ other) - 1) * plan.fwd + part, k_land, bo & (land == me))
-        near = ((lane ^ me) & half) == 0
-        lo_me = lo == me
-        hi_me = hi == me
+        t_fwd = put(t_fwd, e_fwd, ((land ^ other) - 1) * plan.fwd + part, k_land, both & (land == me))
+        lo_me, hi_me = lo == me, hi == me
+        k_both = jnp.where(land == me, k_land, plan.at_fwd + ((land ^ me) - 1) * plan.fwd + part)
+        code = jnp.where(both, k_both, jnp.where(lo_me, k_low, k_high))
+        a, b = row(first, s), row(second, s)
         ok = row(flag(live), s) == 1
-        code_near = (lane ^ me) * cap + jnp.where(lo_me, p_low, p_high)
-        code_fwd = plan.at_fwd + ((land ^ me) - 1) * plan.fwd + part
-        code_far = jnp.where(bo & (land != me), code_fwd, k_land)
-        code = jnp.where(near, code_near, code_far)
-        a, b = row(first, s), row(second, s)
         t_loc = put(t_loc, e_loc, row(w_low, s) * NT + b, code, ok & lo_me)
         t_loc = put(t_loc, e_loc, row(w_high, s) * NT + a, code, ok & hi_me & (a != b))
 
@@ -207,11 +204,7 @@
 
         lax.fori_loop(0, count, one, 0)
         if carries:
-            (f_ref,) = f_refs
-            mine, wide = f_ref.shape
-            for h in range(wide // LANES):
-                at = count * rows * parts + h * mine
-                out[pl.ds(at, mine), :] = f_ref[:, h * LANES : (h + 1) * LANES]
+            write_fock(f_refs[0], out, count * rows * parts)
 
 
 def fock_rows(f_mine):
@@ -240,36 +233,44 @@
     )(table, *[amp] * parts, *f_args)
 
 
-def forward_kernel(plan, soon, size, table_ref, *refs):
-    ins, outs = refs[: plan.half], refs[plan.half :]
+def forward_kernel(plan, size, ranges, table_ref, f_ref, *refs):
+    ins, outs = refs[: len(ranges)], refs[len(ranges) :]
     for k, out in enumerate(outs):
 
         def one(j, carry, k=k, out=out):
             code = table_ref[0, plan.at_fwd + k * plan.fwd + j]
-            for f in range(plan.half):
-                start = (plan.half + f) * plan.cap
-
-                @pl.when((code >= start) & (code < start + soon))
-                def _(f=f, start=start):
+            for ref, (start, count) in zip(ins, ranges):
+
+                @pl.when((code >= start) & (code < start + count))
+                def _(ref=ref, start=start):
                     to, of = pl.multiple_of(j * size, 8), pl.multiple_of((code - start) * size, 8)
-                    out[pl.ds(to, size), :] = ins[f][pl.ds(of, size), :]
+                    out[pl.ds(to, size), :] = ref[pl.ds(of, size), :]
 
             return carry
 
         lax.fori_loop(0, plan.fwd, one, 0)
-
-
-def forward(plan, table, landed, soon, size):
+        write_fock(f_ref, out, plan.fwd * size)
+
+
+def write_fock(f_ref, out, start):
+    mine, wide = f_ref.shape
+    for h in range(wide // LANES):
+        out[pl.ds(start + h * mine, mine), :] = f_ref[:, h * LANES : (h + 1) * LANES]
+
+
+def forward(plan, table, f_mine, landed, ranges, size):
     return pl.pallas_call(
-        functools.partial(forward_kernel, plan, soon, size),
-        out_shape=[jax.ShapeDtypeStruct((plan.fwd * size, LANES), jnp.float32)]
+        functools.partial(forward_kernel, plan, size, ranges),
+        out_shape=[
+            jax.ShapeDtypeStruct((plan.fwd * size + fock_rows(f_mine), LANES), jnp.float32)
+        ]
         * (plan.half - 1),
         in_specs=[pl.BlockSpec(memory_space=pltpu.SMEM)]
-        + [pl.BlockSpec(memory_space=pltpu.VMEM)] * plan.half,
+        + [pl.BlockSpec(memory_space=pltpu.VMEM)] * (1 + len(landed)),
         out_specs=[pl.BlockSpec(memory_space=pltpu.VMEM)] * (plan.half - 1),
         compiler_params=pltpu.CompilerParams(vmem_limit_bytes=VMEM_LIMIT),
         name="forward",
-    )(table, *landed)
+    )(table, f_mine, *landed)
 
 
 def split(x):
@@ -376,22 +377,28 @@
     f_piece = mine, fock_rows(f_mine)
     amp = jnp.transpose(amplitudes, (1, 2, 0, 3)).reshape(tile * tile, slots, occ)
 
-    def branch(wide, soon, table, amp, new_phase, f_mine):
+    def branch(wide, soon, following, table, amp, new_phase, f_mine):
         late = wide - soon
-        far = range(half, nrows)
-        head = pack(table, amp, f_mine, [(k * cap, soon, not late) for k in far])
-        landed = [send(head[k - half], k) for k in far]
-        rest = [(k * cap, cap, True) for k in range(half)]
-        rest += [(k * cap + soon, late, True) for k in far] if late else []
+        side, next_to, far = range(1, plan.quarter), range(plan.quarter, half), range(half, nrows)
+        head = [(k * cap, following, False) for k in next_to]
+        head += [(k * cap, soon, not late) for k in far]
+        head = dict(zip([*next_to, *far], pack(table, amp, f_mine, head)))
+        landed = {k: send(head[k], k) for k in next_to}
+        landed |= {k: send(head[k], k) for k in far}
+        rest = [(k * cap, cap, k == 0) for k in (0, *side)]
+        rest += [(k * cap + soon, late, True) for k in far if late]
         rest = pack(table, amp, f_mine, rest)
-        near_in = [rest[0]] + [send(rest[k], k) for k in range(1, half)]
-        late_in = [send(rest[k], k) for k in far] if late else []
-        relay = forward(plan, table, landed, soon, size)
-        relay_in = [send(x, k + 1) for k, x in enumerate(relay)]
-        buffers = [(k * cap, cap, k, near_in[k]) for k in range(half)]
-        buffers += [(k * cap, soon, None if late else k, landed[k - half]) for k in far]
-        buffers += [(k * cap + soon, late, k, late_in[k - half]) for k in far if late]
-        buffers += [(plan.at_fwd + k * plan.fwd, plan.fwd, None, x) for k, x in enumerate(relay_in)]
+        side_in = {k: send(rest[k], k) for k in side}
+        late_in = {k: send(rest[k - nrows], k) for k in far if late}
+        ranges = [(k * cap, soon if k >= half else following) for k in landed]
+        relay = forward(plan, table, f_mine, list(landed.values()), ranges, size)
+        relay_in = {k: send(relay[k - 1], k) for k in range(1, half)}
+        buffers = [(0, cap, 0, rest[0])]
+        buffers += [(k * cap, cap, None, side_in[k]) for k in side]
+        buffers += [(k * cap, following, None, landed[k]) for k in next_to]
+        buffers += [(k * cap, soon, None if late else k, landed[k]) for k in far]
+        buffers += [(k * cap + soon, late, k, late_in[k]) for k in late_in]
+        buffers += [(plan.at_fwd + (k - 1) * plan.fwd, plan.fwd, k, relay_in[k]) for k in relay_in]
         return contract(plan, table, new_phase, buffers, f_piece, tile, occ)
 
     return lax.switch(

time: 162 us -> 142 us (0.88)
  waiting for transfers between devices: 88 us -> 77.9 us
  starting transfers between devices: 37.4 us -> 28.2 us
    ppermute x14, waiting for transfers between devices: 88 us -> 77.9 us  [send(): return lax.ppermute(x, 'row', [(i, i ^ k) for i in range(nrows)])]
    ppermute x14, starting transfers between devices: 37.4 us -> 28.2 us  [send(): return lax.ppermute(x, 'row', [(i, i ^ k) for i in range(nrows)])]
  transfers between devices with their start and end apart: 14 -> 14, of which waited for: 8 -> 6; matrix products, arithmetic and copies ran while one was open for 2% -> 2% of each run, Pallas kernels for 6% -> 6%
where the time goes in v2:
time: 142 us
  waiting for transfers between devices  77.9 us (55%)
  starting transfers between devices  28.2 us (20%)
  Pallas kernels  26.6 us (19%)
  local copies, waits for them, and re-layouts  7.43 us (5%)
    ppermute x14, waiting for transfers between devices, send(): return lax.ppermute(x, 'row', [(i, i ^ k) for i in range(nrows)])  77.9 us
    ppermute x14, starting transfers between devices, send(): return lax.ppermute(x, 'row', [(i, i ^ k) for i in range(nrows)])  28.2 us
    pallas_call x2, Pallas kernels, pack(): pl.pallas_call(functools.partial(pack_kernel, streams, pad, parts), out_s...  11.1 us
    pallas_call x1, Pallas kernels, contract(): pl.pallas_call(functools.partial(contract_kernel, plan, tile, parts, piec...  10.5 us
    pallas_call x1, Pallas kernels, forward(): pl.pallas_call(functools.partial(forward_kernel, plan, size, ranges), out...  3.24 us
    unnamed x3, local copies, waits for them, and re-layouts  3.07 us
  transfers between devices with their start and end apart: 14, of which 6 were waited for; matrix products, arithmetic and copies ran while one was open for 2% of the time, Pallas kernels for 6%

profile of v2, /device:TPU:0, one launch (start us, length us, event | category | flops | bytes accessed | tf_op | source)
XLA Modules:
  0.0 141.7 jit_solution(4185522000067302642)
XLA Ops:
  0.7 1.4 copy.15
  2.0 1.8 %route.1 = s32[1,128]{1,0:T(1,128)S(1)} custom-call(s32[25,8]{1,0:T(8,128)} %bitcast.28, s32[1,8]{1,0:T(1,128)} %bitcast.29, s32[1]{0:T(128)S(6)} %copy.20.phase_ref), custom_call_target="tpu_custom_call" | custom-call | tf_op jit(solution)/shard_map/route/pallas_call | solution.py:177
  3.8 0.6 slice.3
  5.0 135.0 %conditional.1 = (f32[2,10,160,256]{3,2,1,0:T(8,128)S(1)}) conditional(s32[]{:T(128)} %bitcast.6, (s32[1,128]{1,0:T(1,128)S(1)}, f32[10,10,25,256]{3,2,1,0:T(8,128)}, f32[20,160]{1,0:T(8,128)}, s32[1]{0:T(128)}, ()) %tuple.35, (s32[1,128]{1,0:T(1,128)S(1)}, f32[10,10,25,256]{3,2,1,0:T(8,128)}, f32[20,160]{1,0:T(8,128)}, ...), branch_computations={%region_0.1_spmd, %region_1.2_spmd, %region_2.3_spmd, %region_3.4_... | conditional | bytes 48484720 | solution.py:404
  5.1 0.0 copy-start.21
  5.1 0.0 copy-start
  5.1 6.1 %pack.9 = (f32[1200,128]{1,0:T(8,128)}, f32[1200,128]{1,0:T(8,128)}, f32[600,128]{1,0:T(8,128)}, f32[600,128]{1,0:T(8,128)}, f32[600,128]{1,0:T(8,128)}, /*index=5*/f32[600,128]{1,0:T(8,128)}) custom-call(s32[1,128]{1,0:T(1,128)S(1)} %get-tuple-element.40.table_ref, f32[100,25,256]{2,1,0:T(8,128)} %bitcast.12, f32[100,25,256]{2,1,0:T(8,128)} %bitcast.13), custom_call_target="tpu_custom_call" | custom-call | tf_op jit(solution)/shard_map/cond/branch_0_fun/pack/pallas_call | solution.py:221
  11.2 4.1 %collective-permute-start.3 = (f32[600,128]{1,0:T(8,128)}, f32[600,128]{1,0:T(8,128)}, u32[]{:S(2)}, u32[]{:S(2)}) collective-permute-start(f32[600,128]{1,0:T(8,128)} %get-tuple-element.50), channel_id=1, source_target_pairs={{0,16},{4,20},{8,24},{12,28},{16,0},{20,4},{24,8},{28,12},{1,17},{... | collective-permute-start | bytes 921608 | tf_op jit(solution)/shard_map/cond/branch_0_fun/ppermute | solution.py:371
  15.2 1.3 collective-permute-start.4
  16.5 1.6 %collective-permute-start.1 = (f32[1200,128]{1,0:T(8,128)}, f32[1200,128]{1,0:T(8,128)}, u32[]{:S(2)}, u32[]{:S(2)}) collective-permute-start(f32[1200,128]{1,0:T(8,128)} %get-tuple-element.48), channel_id=1, source_target_pairs={{0,8},{4,12},{8,0},{12,4},{16,24},{20,28},{24,16},{28,20},{1,9},{5... | collective-permute-start | bytes 1843208 | tf_op jit(solution)/shard_map/cond/branch_0_fun/ppermute | solution.py:371
  18.1 0.1 collective-permute-start.2
  18.2 3.9 %collective-permute-start.5 = (f32[600,128]{1,0:T(8,128)}, f32[600,128]{1,0:T(8,128)}, u32[]{:S(2)}, u32[]{:S(2)}) collective-permute-start(f32[600,128]{1,0:T(8,128)} %get-tuple-element.52), channel_id=1, source_target_pairs={{0,24},{4,28},{8,16},{12,20},{16,8},{20,12},{24,0},{28,4},{1,25},{... | collective-permute-start | bytes 921608 | tf_op jit(solution)/shard_map/cond/branch_0_fun/ppermute | solution.py:371
  22.1 14.8 %collective-permute-done.3.refs_2_.refs_4_ = f32[600,128]{1,0:T(8,128)} collective-permute-done((f32[600,128]{1,0:T(8,128)}, f32[600,128]{1,0:T(8,128)}, u32[]{:S(2)}, u32[]{:S(2)}) %collective-permute-start.3) | collective-permute-done | bytes 307232 | tf_op jit(solution)/shard_map/cond/branch_0_fun/ppermute | solution.py:371
  36.9 3.7 %collective-permute-start.6 = (f32[600,128]{1,0:T(8,128)}, f32[600,128]{1,0:T(8,128)}, u32[]{:S(2)}, u32[]{:S(2)}) collective-permute-start(f32[600,128]{1,0:T(8,128)} %get-tuple-element.53), channel_id=1, source_target_pairs={{0,28},{4,24},{8,20},{12,16},{16,12},{20,8},{24,4},{28,0},{1,29},{... | collective-permute-start | bytes 921608 | tf_op jit(solution)/shard_map/cond/branch_0_fun/ppermute | solution.py:371
  40.7 0.0 copy-done.21
  40.7 0.8 reshape.27
  41.4 0.9 pad.5
  42.4 0.7 reshape.23.refs_2_.f_ref
  43.1 0.0 copy-done
  43.1 5.0 %pack.8 = (f32[1640,128]{1,0:T(8,128)}, f32[1600,128]{1,0:T(8,128)}, f32[440,128]{1,0:T(8,128)}, f32[440,128]{1,0:T(8,128)}, f32[440,128]{1,0:T(8,128)}, /*index=5*/f32[440,128]{1,0:T(8,128)}) custom-call(s32[1,128]{1,0:T(1,128)S(1)} %get-tuple-element.40.table_ref, f32[100,25,256]{2,1,0:T(8,128)S(1)} %bitcast.14, f32[100,25,256]{2,1,0:T(8,128)S(1)} %bitcast.15, ...), custom_call_target="tpu_custom_call" | custom-call | tf_op jit(solution)/shard_map/cond/branch_0_fun/pack/pallas_call | solution.py:221
  48.1 0.0 collective-permute-done.4.refs_3_.refs_5_
  48.1 0.5 collective-permute-start
  48.6 20.3 %collective-permute-done.5.refs_4_.refs_6_ = f32[600,128]{1,0:T(8,128)} collective-permute-done((f32[600,128]{1,0:T(8,128)}, f32[600,128]{1,0:T(8,128)}, u32[]{:S(2)}, u32[]{:S(2)}) %collective-permute-start.5) | collective-permute-done | bytes 307232 | tf_op jit(solution)/shard_map/cond/branch_0_fun/ppermute | solution.py:371
  68.9 0.0 collective-permute-start.7
  68.9 6.8 %collective-permute-done.6.refs_5_.refs_7_ = f32[600,128]{1,0:T(8,128)} collective-permute-done((f32[600,128]{1,0:T(8,128)}, f32[600,128]{1,0:T(8,128)}, u32[]{:S(2)}, u32[]{:S(2)}) %collective-permute-start.6) | collective-permute-done | bytes 307232 | tf_op jit(solution)/shard_map/cond/branch_0_fun/ppermute | solution.py:371
  75.7 0.0 collective-permute-start.8
  75.7 0.0 collective-permute-done.1.refs_0_.refs_2_
  75.7 5.2 %collective-permute-start.9 = (f32[440,128]{1,0:T(8,128)}, f32[440,128]{1,0:T(8,128)S(1)}, u32[]{:S(2)}, u32[]{:S(2)}) collective-permute-start(f32[440,128]{1,0:T(8,128)} %get-tuple-element.56), channel_id=1, source_target_pairs={{0,24},{4,28},{8,16},{12,20},{16,8},{20,12},{24,0},{28,4},{1,25},{... | collective-permute-start | bytes 675848 | tf_op jit(solution)/shard_map/cond/branch_0_fun/ppermute | solution.py:371
  80.9 0.0 collective-permute-done.2.refs_1_.refs_3_
  80.9 3.2 %forward.4 = (f32[840,128]{1,0:T(8,128)}, f32[840,128]{1,0:T(8,128)}, f32[840,128]{1,0:T(8,128)}) custom-call(s32[1,128]{1,0:T(1,128)S(1)} %get-tuple-element.40.table_ref, f32[20,256]{1,0:T(8,128)} %reshape.23.refs_2_.f_ref, f32[1200,128]{1,0:T(8,128)} %collective-permute-done.1.refs_0_.refs_2_, f32[1200,128]{1,0:T(8,128)} %collective-permute-done.2.refs_1_.refs_3_, ...), custom_call_target="tpu_custom_call" | custom-call | tf_op jit(solution)/shard_map/cond/branch_0_fun/forward/pallas_call | solution.py:262
  84.1 0.4 collective-permute-start.11
  84.6 8.3 %collective-permute-done.7.refs_8_ = f32[440,128]{1,0:T(8,128)S(1)} collective-permute-done((f32[440,128]{1,0:T(8,128)}, f32[440,128]{1,0:T(8,128)S(1)}, u32[]{:S(2)}, u32[]{:S(2)}) %collective-permute-start.7) | collective-permute-done | bytes 225312 | tf_op jit(solution)/shard_map/cond/branch_0_fun/ppermute | solution.py:371
  92.9 2.3 %collective-permute-start.12 = (f32[840,128]{1,0:T(8,128)}, f32[840,128]{1,0:T(8,128)S(1)}, u32[]{:S(2)}, u32[]{:S(2)}) collective-permute-start(f32[840,128]{1,0:T(8,128)} %get-tuple-element.59), channel_id=1, source_target_pairs={{0,8},{4,12},{8,0},{12,4},{16,24},{20,28},{24,16},{28,20},{1,9},{5... | collective-permute-start | bytes 1290248 | tf_op jit(solution)/shard_map/cond/branch_0_fun/ppermute | solution.py:371
  95.2 3.5 %collective-permute-done.8.refs_9_ = f32[440,128]{1,0:T(8,128)S(1)} collective-permute-done((f32[440,128]{1,0:T(8,128)}, f32[440,128]{1,0:T(8,128)S(1)}, u32[]{:S(2)}, u32[]{:S(2)}) %collective-permute-start.8) | collective-permute-done | bytes 225312 | tf_op jit(solution)/shard_map/cond/branch_0_fun/ppermute | solution.py:371
  98.7 2.4 %collective-permute-start.13 = (f32[840,128]{1,0:T(8,128)}, f32[840,128]{1,0:T(8,128)S(1)}, u32[]{:S(2)}, u32[]{:S(2)}) collective-permute-start(f32[840,128]{1,0:T(8,128)} %get-tuple-element.60), channel_id=1, source_target_pairs={{0,12},{4,8},{8,4},{12,0},{16,28},{20,24},{24,20},{28,16},{1,13},{... | collective-permute-start | bytes 1290248 | tf_op jit(solution)/shard_map/cond/branch_0_fun/ppermute | solution.py:371
  101.1 0.0 collective-permute-done.9.refs_10_
  101.1 2.7 %collective-permute-start.10 = (f32[440,128]{1,0:T(8,128)}, f32[440,128]{1,0:T(8,128)S(1)}, u32[]{:S(2)}, u32[]{:S(2)}) collective-permute-start(f32[440,128]{1,0:T(8,128)} %get-tuple-element.57), channel_id=1, source_target_pairs={{0,28},{4,24},{8,20},{12,16},{16,12},{20,8},{24,4},{28,0},{1,29},{... | collective-permute-start | bytes 675848 | tf_op jit(solution)/shard_map/cond/branch_0_fun/ppermute | solution.py:371
  103.8 24.1 %collective-permute-done.10.refs_11_ = f32[440,128]{1,0:T(8,128)S(1)} collective-permute-done((f32[440,128]{1,0:T(8,128)}, f32[440,128]{1,0:T(8,128)S(1)}, u32[]{:S(2)}, u32[]{:S(2)}) %collective-permute-start.10) | collective-permute-done | bytes 225312 | tf_op jit(solution)/shard_map/cond/branch_0_fun/ppermute | solution.py:371
  127.9 0.0 collective-permute-done.refs_1_
  127.9 0.0 collective-permute-done.11.refs_12_
  127.9 0.0 copy-start.12
  127.9 0.0 collective-permute-done.12.refs_13_
  127.9 0.0 collective-permute-done.13.refs_14_
  128.0 1.1 copy-done.31
  129.1 0.2 copy-done.5
  129.3 10.5 %contract.4 = f32[2,10,160,256]{3,2,1,0:T(8,128)S(1)} custom-call(s32[1,128]{1,0:T(1,128)S(1)} %get-tuple-element.40.table_ref, s32[1]{0:T(128)} %get-tuple-element.42.phase_ref, f32[1640,128]{1,0:T(8,128)} %get-tuple-element.46.refs_0_, f32[1600,128]{1,0:T(8,128)} %copy-done.5, f32[1200,128]{1,0:T(8,128)} %collective-permute-done.1.refs_0_.refs_2_, ...), custom_call_target="tpu_custom_call" | custom-call | tf_op jit(solution)/shard_map/cond/branch_0_fun/contract/pallas_call | solution.py:341
  140.0 0.0 copy-start.4
  140.0 1.7 %copy-done.4 = f32[2,10,160,256]{3,2,1,0:T(8,128)} copy-done((f32[2,10,160,256]{3,2,1,0:T(8,128)}, f32[2,10,160,256]{3,2,1,0:T(8,128)S(1)}, u32[]{:S(2)}) %copy-start.4) | copy-done | bytes 3276824
  (13 shorter events, 0.0 us)
Async XLA Ops:
  5.1 35.6 %copy-start.21 = (f32[20,160]{1,0:T(8,128)S(1)}, f32[20,160]{1,0:T(8,128)}, u32[]{:S(2)}) copy-start(f32[20,160]{1,0:T(8,128)} %get-tuple-element.139) | copy-start | bytes 38404 | tf_op jit(solution)/shard_map/cond
  5.1 38.0 %copy-start = (f32[10,10,25,256]{3,2,1,0:T(8,128)S(1)}, f32[10,10,25,256]{3,2,1,0:T(8,128)}, u32[]{:S(2)}) copy-start(f32[10,10,25,256]{3,2,1,0:T(8,128)} %get-tuple-element.115) | copy-start | bytes 7680004 | tf_op jit(solution)/shard_map/cond
  11.2 25.8 %collective-permute-start.3 = (f32[600,128]{1,0:T(8,128)}, f32[600,128]{1,0:T(8,128)}, u32[]{:S(2)}, u32[]{:S(2)}) collective-permute-start(f32[600,128]{1,0:T(8,128)} %get-tuple-element.50), channel_id=1, source_target_pairs={{0,16},{4,20},{8,24},{12,28},{16,0},{20,4},{24,8},{28,12},{1,17},{... | collective-permute-start | bytes 921608 | tf_op jit(solution)/shard_map/cond/branch_0_fun/ppermute | solution.py:371
  15.2 32.9 %collective-permute-start.4 = (f32[600,128]{1,0:T(8,128)}, f32[600,128]{1,0:T(8,128)}, u32[]{:S(2)}, u32[]{:S(2)}) collective-permute-start(f32[600,128]{1,0:T(8,128)} %get-tuple-element.51), channel_id=1, source_target_pairs={{0,20},{4,16},{8,28},{12,24},{16,4},{20,0},{24,12},{28,8},{1,21},{... | collective-permute-start | bytes 921608 | tf_op jit(solution)/shard_map/cond/branch_0_fun/ppermute | solution.py:371
  16.5 59.2 %collective-permute-start.1 = (f32[1200,128]{1,0:T(8,128)}, f32[1200,128]{1,0:T(8,128)}, u32[]{:S(2)}, u32[]{:S(2)}) collective-permute-start(f32[1200,128]{1,0:T(8,128)} %get-tuple-element.48), channel_id=1, source_target_pairs={{0,8},{4,12},{8,0},{12,4},{16,24},{20,28},{24,16},{28,20},{1,9},{5... | collective-permute-start | bytes 1843208 | tf_op jit(solution)/shard_map/cond/branch_0_fun/ppermute | solution.py:371
  18.1 62.8 %collective-permute-start.2 = (f32[1200,128]{1,0:T(8,128)}, f32[1200,128]{1,0:T(8,128)}, u32[]{:S(2)}, u32[]{:S(2)}) collective-permute-start(f32[1200,128]{1,0:T(8,128)} %get-tuple-element.49), channel_id=1, source_target_pairs={{0,12},{4,8},{8,4},{12,0},{16,28},{20,24},{24,20},{28,16},{1,13},{... | collective-permute-start | bytes 1843208 | tf_op jit(solution)/shard_map/cond/branch_0_fun/ppermute | solution.py:371
  18.2 50.7 %collective-permute-start.5 = (f32[600,128]{1,0:T(8,128)}, f32[600,128]{1,0:T(8,128)}, u32[]{:S(2)}, u32[]{:S(2)}) collective-permute-start(f32[600,128]{1,0:T(8,128)} %get-tuple-element.52), channel_id=1, source_target_pairs={{0,24},{4,28},{8,16},{12,20},{16,8},{20,12},{24,0},{28,4},{1,25},{... | collective-permute-start | bytes 921608 | tf_op jit(solution)/shard_map/cond/branch_0_fun/ppermute | solution.py:371
  36.9 38.8 %collective-permute-start.6 = (f32[600,128]{1,0:T(8,128)}, f32[600,128]{1,0:T(8,128)}, u32[]{:S(2)}, u32[]{:S(2)}) collective-permute-start(f32[600,128]{1,0:T(8,128)} %get-tuple-element.53), channel_id=1, source_target_pairs={{0,28},{4,24},{8,20},{12,16},{16,12},{20,8},{24,4},{28,0},{1,29},{... | collective-permute-start | bytes 921608 | tf_op jit(solution)/shard_map/cond/branch_0_fun/ppermute | solution.py:371
  48.1 79.8 %collective-permute-start = (f32[1600,128]{1,0:T(8,128)}, f32[1600,128]{1,0:T(8,128)S(1)}, u32[]{:S(2)}, u32[]{:S(2)}) collective-permute-start(f32[1600,128]{1,0:T(8,128)} %get-tuple-element.47), channel_id=1, source_target_pairs={{0,4},{4,0},{8,12},{12,8},{16,20},{20,16},{24,28},{28,24},{1,5},{5... | collective-permute-start | bytes 2457608 | tf_op jit(solution)/shard_map/cond/branch_0_fun/ppermute | solution.py:371
  68.9 24.0 %collective-permute-start.7 = (f32[440,128]{1,0:T(8,128)}, f32[440,128]{1,0:T(8,128)S(1)}, u32[]{:S(2)}, u32[]{:S(2)}) collective-permute-start(f32[440,128]{1,0:T(8,128)} %get-tuple-element.54), channel_id=1, source_target_pairs={{0,16},{4,20},{8,24},{12,28},{16,0},{20,4},{24,8},{28,12},{1,17},{... | collective-permute-start | bytes 675848 | tf_op jit(solution)/shard_map/cond/branch_0_fun/ppermute | solution.py:371
  75.7 23.0 %collective-permute-start.8 = (f32[440,128]{1,0:T(8,128)}, f32[440,128]{1,0:T(8,128)S(1)}, u32[]{:S(2)}, u32[]{:S(2)}) collective-permute-start(f32[440,128]{1,0:T(8,128)} %get-tuple-element.55), channel_id=1, source_target_pairs={{0,20},{4,16},{8,28},{12,24},{16,4},{20,0},{24,12},{28,8},{1,21},{... | collective-permute-start | bytes 675848 | tf_op jit(solution)/shard_map/cond/branch_0_fun/ppermute | solution.py:371
  75.7 25.4 %collective-permute-start.9 = (f32[440,128]{1,0:T(8,128)}, f32[440,128]{1,0:T(8,128)S(1)}, u32[]{:S(2)}, u32[]{:S(2)}) collective-permute-start(f32[440,128]{1,0:T(8,128)} %get-tuple-element.56), channel_id=1, source_target_pairs={{0,24},{4,28},{8,16},{12,20},{16,8},{20,12},{24,0},{28,4},{1,25},{... | collective-permute-start | bytes 675848 | tf_op jit(solution)/shard_map/cond/branch_0_fun/ppermute | solution.py:371
  84.1 43.8 %collective-permute-start.11 = (f32[840,128]{1,0:T(8,128)}, f32[840,128]{1,0:T(8,128)S(1)}, u32[]{:S(2)}, u32[]{:S(2)}) collective-permute-start(f32[840,128]{1,0:T(8,128)} %get-tuple-element.58), channel_id=1, source_target_pairs={{0,4},{4,0},{8,12},{12,8},{16,20},{20,16},{24,28},{28,24},{1,5},{5... | collective-permute-start | bytes 1290248 | tf_op jit(solution)/shard_map/cond/branch_0_fun/ppermute | solution.py:371
  92.9 35.1 %copy-start.28 = (f32[440,128]{1,0:T(8,128)}, f32[440,128]{1,0:T(8,128)S(1)}, u32[]{:S(2)}) copy-start(f32[440,128]{1,0:T(8,128)S(1)} %collective-permute-done.7.refs_8_) | copy-start | bytes 675844 | tf_op jit(solution)/shard_map/cond
  92.9 35.0 %collective-permute-start.12 = (f32[840,128]{1,0:T(8,128)}, f32[840,128]{1,0:T(8,128)S(1)}, u32[]{:S(2)}, u32[]{:S(2)}) collective-permute-start(f32[840,128]{1,0:T(8,128)} %get-tuple-element.59), channel_id=1, source_target_pairs={{0,8},{4,12},{8,0},{12,4},{16,24},{20,28},{24,16},{28,20},{1,9},{5... | collective-permute-start | bytes 1290248 | tf_op jit(solution)/shard_map/cond/branch_0_fun/ppermute | solution.py:371
  98.7 29.3 %copy-start.29 = (f32[440,128]{1,0:T(8,128)}, f32[440,128]{1,0:T(8,128)S(1)}, u32[]{:S(2)}) copy-start(f32[440,128]{1,0:T(8,128)S(1)} %collective-permute-done.8.refs_9_) | copy-start | bytes 675844 | tf_op jit(solution)/shard_map/cond
  98.7 29.2 %collective-permute-start.13 = (f32[840,128]{1,0:T(8,128)}, f32[840,128]{1,0:T(8,128)S(1)}, u32[]{:S(2)}, u32[]{:S(2)}) collective-permute-start(f32[840,128]{1,0:T(8,128)} %get-tuple-element.60), channel_id=1, source_target_pairs={{0,12},{4,8},{8,4},{12,0},{16,28},{20,24},{24,20},{28,16},{1,13},{... | collective-permute-start | bytes 1290248 | tf_op jit(solution)/shard_map/cond/branch_0_fun/ppermute | solution.py:371
  101.1 26.9 %copy-start.30 = (f32[440,128]{1,0:T(8,128)}, f32[440,128]{1,0:T(8,128)S(1)}, u32[]{:S(2)}) copy-start(f32[440,128]{1,0:T(8,128)S(1)} %collective-permute-done.9.refs_10_) | copy-start | bytes 675844 | tf_op jit(solution)/shard_map/cond
  101.1 26.8 %collective-permute-start.10 = (f32[440,128]{1,0:T(8,128)}, f32[440,128]{1,0:T(8,128)S(1)}, u32[]{:S(2)}, u32[]{:S(2)}) collective-permute-start(f32[440,128]{1,0:T(8,128)} %get-tuple-element.57), channel_id=1, source_target_pairs={{0,28},{4,24},{8,20},{12,16},{16,12},{20,8},{24,4},{28,0},{1,29},{... | collective-permute-start | bytes 675848 | tf_op jit(solution)/shard_map/cond/branch_0_fun/ppermute | solution.py:371
  127.9 1.2 copy-start.31
  127.9 1.4 copy-start.5
  127.9 1.1 copy-start.12
  127.9 1.1 copy-start.14
  128.0 1.1 copy-start.16
  140.0 1.7 %copy-start.4 = (f32[2,10,160,256]{3,2,1,0:T(8,128)}, f32[2,10,160,256]{3,2,1,0:T(8,128)S(1)}, u32[]{:S(2)}) copy-start(f32[2,10,160,256]{3,2,1,0:T(8,128)S(1)} %get-tuple-element.147) | copy-start | bytes 9830404
